TPU v7x, 8 devices: a whole 2x2x1 slice. The times are simulated.
8 devices in a mesh: fsdp: 8 (over z, y, x, core).
Axes of the slice: x: 2, y: 2, z: 1, core: 2. Of those that a mesh axis runs over, the one named last changes fastest.
Arguments:
- hidden: bfloat16 [16, 1024, 2048], P('fsdp')
- norm_gain: bfloat16 [2048], P('fsdp')
- w_head: bfloat16 [32000, 2048], P('fsdp')
- labels: int32 [16, 1024], P('fsdp')
Outputs:
- output 1: float32 [], replicated
- output 2: bfloat16 [16, 1024, 2048], P('fsdp')
- output 3: float32 [32000, 2048], P('fsdp')
- output 4: float32 [2048], P('fsdp')
All inputs are finite; a program needn't handle non-finite values.
Results may differ from a plain program's by a relative error of at most 0.00857454.
Values are sent between devices in bfloat16 or wider.
A program may use at most 1 GiB of HBM per device.

v0:
```python
import jax
import jax.numpy as jnp
from jax import lax
from jax.sharding import PartitionSpec as P

EPSILON = 1e-5


def solution(mesh):
    def local_step(hidden, norm_gain, w_head, labels):
        full_w = lax.all_gather(w_head, 'fsdp', axis=0, tiled=True)
        full_g = lax.all_gather(norm_gain, 'fsdp', axis=0, tiled=True)
        batch_rows, seq_len, hidden_dim = hidden.shape
        tok_lab = labels.reshape(batch_rows * seq_len)
        is_valid = tok_lab >= 0
        tok_count = lax.psum(jnp.sum(is_valid.astype(jnp.float32)), 'fsdp')
        h_f32 = hidden.reshape(batch_rows * seq_len, hidden_dim).astype(jnp.float32)
        inv_rms = lax.rsqrt(jnp.mean(h_f32 * h_f32, axis=-1, keepdims=True) + EPSILON)
        normed = (h_f32 * inv_rms).astype(jnp.bfloat16)
        gain_f32 = full_g.astype(jnp.float32)
        x_in = (normed.astype(jnp.float32) * gain_f32).astype(jnp.bfloat16)
        logits = jnp.einsum('td,vd->tv', x_in, full_w, preferred_element_type=jnp.float32)
        row_max = jnp.max(logits, axis=-1, keepdims=True)
        shifted = jnp.exp(logits - row_max)
        sum_exp = jnp.sum(shifted, axis=-1, keepdims=True)
        log_norm = row_max[:, 0] + jnp.log(sum_exp[:, 0])
        vocab_ids = lax.broadcasted_iota(jnp.int32, (1, full_w.shape[0]), 1)
        onehot = vocab_ids == tok_lab[:, None]
        picked = jnp.sum(jnp.where(onehot, logits, 0.0), axis=-1)
        loss_value = lax.psum(jnp.sum(jnp.where(is_valid, log_norm - picked, 0.0)), 'fsdp') / tok_count
        dlog_bf = (jnp.where(is_valid[:, None], shifted / sum_exp - onehot.astype(jnp.float32), 0.0) / tok_count).astype(jnp.bfloat16)
        grad_x = jnp.einsum('tv,vd->td', dlog_bf, full_w, preferred_element_type=jnp.float32).astype(jnp.bfloat16)
        dw_full = jnp.einsum('tv,td->vd', dlog_bf, x_in, preferred_element_type=jnp.float32)
        grad_w = lax.psum_scatter(dw_full, 'fsdp', scatter_dimension=0, tiled=True)
        gx_f32 = grad_x.astype(jnp.float32)
        dg_full = jnp.sum(gx_f32 * normed.astype(jnp.float32), axis=0)
        grad_g = lax.psum_scatter(dg_full, 'fsdp', scatter_dimension=0, tiled=True)
        grad_n = gx_f32 * gain_f32
        dot_proj = jnp.mean(grad_n * h_f32, axis=-1, keepdims=True)
        grad_h = (inv_rms * grad_n - h_f32 * inv_rms ** 3 * dot_proj).astype(jnp.bfloat16)
        return loss_value, grad_h.reshape(batch_rows, seq_len, hidden_dim), grad_w, grad_g

    return jax.shard_map(local_step, mesh=mesh, in_specs=(P('fsdp', None, None), P('fsdp'), P('fsdp', None), P('fsdp', None)), out_specs=(P(), P('fsdp', None, None), P('fsdp', None), P('fsdp')), check_vma=False)
```

profile of v0, /device:TPU:0, one launch (start us, length us, event | category | flops | bytes accessed | tf_op | source)
XLA Modules:
  0.0 2832.1 jit_solution(8238281063425716485)
XLA Ops:
  7.2 0.0 copy-start.11
  7.2 0.0 copy-start.3
  7.2 0.0 all-gather.3.cloned.1.call-start
  7.2 0.7 all-gather.3.cloned.1.call-update
  7.9 0.0 reduce-scatter.4.cloned.1.call-start
  8.0 5.1 fusion.8
  13.1 0.0 copy-start.5
  13.1 0.0 copy-done.11
  13.1 0.0 copy-start.1
  13.1 13.5 all-gather
  26.7 0.0 copy-start.7
  26.7 0.0 copy-done.3
  26.7 0.6 copy.16
  27.3 0.6 broadcast_compare_fusion
  27.9 0.0 copy-done.5
  27.9 0.0 copy-done.1
  27.9 8.2 fusion.9
  36.1 544.4 %all-gather.3.cloned.1.call-done = bf16[32000,2048]{1,0:T(8,128)(2,1)} async-done(((bf16[4000,2048]{1,0:T(8,128)(2,1)}), bf16[32000,2048]{1,0:T(8,128)(2,1)}) %all-gather.3.cloned.1.call-update) | async-done | bytes 131072016 | tf_op jit(solution)/shard_map/all_gather | solution.py:11
  580.6 0.0 copy-start
  580.6 292.0 %fusion.15 = (f32[2048]{0:T(1024)S(1)}, f32[2048,32000]{1,0:T(8,128)}) fusion(bf16[32000,2048]{1,0:T(8,128)(2,1)} %all-gather.3.cloned.1.call-done, bf16[2048,2048]{1,0:T(8,128)(2,1)} %fusion.9, f32[2048]{0:T(1024)S(1)} %bitcast.38), kind=kOutput, calls=%fused_computation.34 | convolution fusion | flops 268513574912 | bytes 401620992 | tf_op jit(solution)/shard_map/td,vd->tv/dot_general | solution.py:22
  872.5 0.0 copy-done.7
  872.5 0.0 copy-done
  872.5 0.0 copy-start.4
  872.5 0.0 copy-start.10
  872.5 94.1 %fusion = (f32[2048]{0:T(1024)S(1)}, f32[2048]{0:T(1024)S(1)}) fusion(f32[2048,32000]{1,0:T(8,128)} %get-tuple-element.13, f32[2048]{0:T(1024)S(1)} %get-tuple-element.12, s32[2048]{0:T(1024)S(1)} %bitcast.32), kind=kLoop, calls=%fused_computation.4 | loop fusion | flops 327675904 | bytes 262176768 | tf_op jit(solution)/shard_map/reduce_sum | solution.py:25
  966.7 0.0 copy-done.4
  966.7 0.6 convert_reduce_fusion
  967.3 22.4 psum.15
  989.8 0.0 copy-done.10
  989.8 0.0 copy-start.8
  989.8 125.1 %divide_convert_fusion = bf16[2048,32000]{1,0:T(8,128)(2,1)} fusion(f32[2048,32000]{1,0:T(8,128)} %get-tuple-element.13, f32[]{:T(128)} %psum.15, f32[2048]{0:T(1024)S(1)} %get-tuple-element.4, s32[2048]{0:T(1024)S(1)} %bitcast.33, f32[2048]{0:T(1024)S(1)} %get-tuple-element.12, pred[2048]{0:T(1024)(128)(4,1)S(1)} %copy-done.10), kind=kLoop, calls=%fused_computation | loop fusion | flops 524288000 | bytes 393242624 | tf_op jit(solution)/shard_map/convert_element_type | solution.py:31
  1114.8 0.0 copy-done.8
  1114.8 288.0 %fusion.11 = f32[32000,2048]{1,0:T(8,128)} fusion(bf16[2048,32000]{1,0:T(8,128)(2,1)} %divide_convert_fusion, bf16[2048,2048]{1,0:T(8,128)(2,1)} %fusion.9, f32[2048]{0:T(1024)S(1)} %bitcast.39), kind=kOutput, calls=%fused_computation.22 | convolution fusion | flops 268448038912 | bytes 401612800 | tf_op jit(solution)/shard_map/tv,td->vd/dot_general | solution.py:33
  1402.8 0.0 copy-start.6
  1402.8 0.0 reduce-scatter.4.cloned.1.call-update
  1402.9 0.7 copy-done.6
  1403.5 0.6 multiply_multiply_fusion
  1404.1 0.0 copy-start.2
  1404.1 0.0 copy-start.9
  1404.1 293.0 %fusion.7 = (f32[2048]{0:T(1024)S(1)}, f32[2048]{0:T(1024)S(1)}, bf16[2048,2048]{1,0:T(8,128)(2,1)}) fusion(bf16[2048,2048]{1,0:T(8,128)(2,1)} %fusion.9, bf16[2,1024,2048]{2,1,0:T(8,128)(2,1)} %param.4, f32[2048]{0:T(1024)S(1)} %bitcast.40, bf16[2048,32000]{1,0:T(8,128)(2,1)} %divide_convert_fusion, bf16[32000,2048]{1,0:T(8,128)(2,1)} %all-gather.3.cloned.1.call-done), kind=kOutput, calls=%fused_computation.14 | convolution fusion | flops 268473204736 | bytes 287334400 | tf_op jit(solution)/shard_map/tv,vd->td/dot_general | solution.py:32
  1697.1 24.3 all-reduce.2
  1722.8 0.6 dynamic-slice.1
  1723.4 0.0 copy-done.2
  1723.4 0.0 copy-done.9
  1723.4 10.8 fusion.4
  1734.2 1089.5 %reduce-scatter.4.cloned.1.call-done = f32[4000,2048]{1,0:T(8,128)} async-done(((f32[32000,2048]{1,0:T(8,128)}), f32[4000,2048]{1,0:T(8,128)}) %reduce-scatter.4.cloned.1.call-update) | async-done | bytes 32768016
  (7 shorter events, 0.1 us)
Async XLA Ops:
  7.2 5.9 copy-start.11
  7.2 19.5 copy-start.3
  7.2 573.4 %all-gather.3.cloned.1.call-start = ((), (), s32[]{:S(2)}) async-start(), calls=%async_computation.1 | async-start | bytes 147456000 | tf_op jit(solution)/shard_map/all_gather | solution.py:11
  7.9 2815.7 %reduce-scatter.4.cloned.1.call-start = ((), (), s32[]{:S(2)}) async-start(), calls=%async_computation.2 | async-start | bytes 294912000
  13.1 14.8 copy-start.5
  13.1 14.8 copy-start.1
  26.7 845.8 %copy-start.7 = (f32[8,1,256]{2,1,0:T(1,128)}, f32[8,1,256]{2,1,0:T(1,128)S(1)}, u32[]{:S(2)}) copy-start(f32[8,1,256]{2,1,0:T(1,128)S(1)} %convert_element_type.55) | copy-start | bytes 24580
  580.6 292.0 %copy-start = (s32[1,8,2,128]{3,1,2,0:T(8,128)S(1)}, s32[1,8,2,128]{3,1,2,0:T(8,128)}, u32[]{:S(2)}) copy-start(s32[1,8,2,128]{3,1,2,0:T(8,128)} %copy.16) | copy-start | bytes 24580
  872.5 94.2 %copy-start.4 = (s32[2,1024]{1,0:T(2,128)S(1)}, s32[2,1024]{1,0:T(2,128)}, u32[]{:S(2)}) copy-start(s32[2,1024]{1,0:T(2,128)} %param.7) | copy-start | bytes 24580
  872.5 117.2 %copy-start.10 = (pred[2048]{0:T(1024)(128)(4,1)S(1)}, pred[2048]{0:T(1024)(128)(4,1)}, u32[]{:S(2)}) copy-start(pred[2048]{0:T(1024)(128)(4,1)} %broadcast_compare_fusion) | copy-start | bytes 6148
  989.8 125.1 %copy-start.8 = (f32[8,1,256]{2,1,0:T(1,128)S(1)}, f32[8,1,256]{2,1,0:T(1,128)}, u32[]{:S(2)}) copy-start(f32[8,1,256]{2,1,0:T(1,128)} %copy-done.7) | copy-start | bytes 24580
  1402.8 0.7 copy-start.6
  1404.1 319.3 %copy-start.2 = (f32[1,8,2,128]{3,1,2,0:T(8,128)S(1)}, f32[1,8,2,128]{3,1,2,0:T(8,128)}, u32[]{:S(2)}) copy-start(f32[1,8,2,128]{3,1,2,0:T(8,128)} %copy-done.1) | copy-start | bytes 24580
  1404.1 319.3 %copy-start.9 = (f32[2048]{0:T(1024)S(1)}, f32[2048]{0:T(1024)}, u32[]{:S(2)}) copy-start(f32[2048]{0:T(1024)} %multiply_multiply_fusion) | copy-start | bytes 24580
Sparse Core Ops, SparseCore 0:
  9.8 570.6 all-gather.2
  1403.0 1420.6 reduce-scatter.3
where the time goes:
time: 2840 us; the launch traced here: 2830 us
  waiting for transfers between devices  1630 us (57%)
  matrix products  873 us (31%)
  other arithmetic  245 us (9%)
  blocking collectives  60.3 us (2%)
    unnamed x3, waiting for transfers between devices  1090 us
    all_gather x1, waiting for transfers between devices, local_step(): full_w = lax.all_gather(w_head, 'fsdp', axis=0, tiled=True)  544 us
    dot_general x1, matrix products, local_step(): jnp.einsum('tv,vd->td', dlog_bf, full_w, preferred_element_type=jnp.float32)  293 us
    dot_general x1, matrix products, local_step(): jnp.einsum('td,vd->tv', x_in, full_w, preferred_element_type=jnp.float32)  292 us
    dot_general x1, matrix products, local_step(): jnp.einsum('tv,td->vd', dlog_bf, x_in, preferred_element_type=jnp.float32)  288 us
    convert_element_type x1, other arithmetic, local_step(): (jnp.where(is_valid[:, None], shifted / sum_exp - onehot.astype(jnp.float...  125 us
    reduce_sum x1, other arithmetic, local_step(): sum_exp = jnp.sum(shifted, axis=-1, keepdims=True)  94.1 us
  transfers between devices with their start and end apart: 2, of which 2 were waited for; matrix products, arithmetic and copies ran while one was open for 11% of the time, Pallas kernels for 0%

commit v1 on v0

v1 whole, which is shorter than its diff:
```python
import functools

import jax
import jax.numpy as jnp
from jax import lax
from jax.experimental import pallas as pl
from jax.experimental.pallas import tpu as pltpu
from jax.sharding import PartitionSpec as P


EPSILON = 1e-5

AX = "fsdp"
NDEV = 8
D = 2048
VD = 4000
VC = 8000
CH = 512
HF = CH // 2
NCH = 4
VB1 = 800
VB2 = 1000
SUB = 80
F32 = jnp.float32
BF16 = jnp.bfloat16
VMEM_LIMIT = 63 * 2 ** 20
NB1 = VC // VB1
NB2 = VC // VB2


def logits_kernel(moves, aliased, ndep, core_ref, w_ref, *refs):
    nx = len(moves)
    xs, refs = refs[:nx], refs[nx + ndep + (1 if aliased else 0):]
    l_ref, lse_ref, x_all, x_ref, m_ref, s_ref, sems = refs
    v = pl.program_id(0)
    flat = [(x, mv) for x, mvs in zip(xs, moves) for mv in mvs]
    loads = [pltpu.make_async_copy(x.at[pl.ds(a, n), :], x_ref.at[pl.ds(b, n), :], sems.at[0, i]) for i, (x, (a, b, _, n)) in enumerate(flat)]
    saves = [pltpu.make_async_copy(x_ref.at[pl.ds(b, n), :], x_all.at[pl.ds(g, n), :], sems.at[1, i]) for i, (_, (_, b, g, n)) in enumerate(flat)]

    @pl.when(v == 0)
    def _():
        for cp in loads:
            cp.start()
        m_ref[...] = jnp.full_like(m_ref, -jnp.inf)
        s_ref[...] = jnp.zeros_like(s_ref)
        for cp in loads:
            cp.wait()
        for cp in saves:
            cp.start()

    l = lax.dot_general(w_ref[...], x_ref[...], (((1,), (1,)), ((), ())), preferred_element_type=F32)
    l_ref[...] = l
    m, s = m_ref[...], s_ref[...]
    for q in range(VB1 // SUB):
        blk = l[q * SUB:(q + 1) * SUB]
        m_new = jnp.maximum(m, jnp.max(blk, axis=0, keepdims=True))
        s = s * jnp.exp(m - m_new) + jnp.sum(jnp.exp(blk - m_new), axis=0, keepdims=True)
        m = m_new
    m_ref[...] = m
    s_ref[...] = s

    @pl.when(v == pl.num_programs(0) - 1)
    def _():
        lse_ref[...] = m_ref[...] + jnp.log(s_ref[...])
        for cp in saves:
            cp.wait()


def local_logits(core, w, xs, moves, x_all, deps):
    t = NCH * CH
    half = NB1 // 2
    nmv = sum(len(m) for m in moves)
    anywhere = pl.BlockSpec(memory_space=pl.ANY)
    args = [core, w, *xs, *deps]
    aliases = {}
    if x_all is not None:
        aliases = {len(args): 2}
        args.append(x_all)
    return pl.pallas_call(
        functools.partial(logits_kernel, moves, x_all is not None, len(deps)),
        grid_spec=pltpu.PrefetchScalarGridSpec(
            num_scalar_prefetch=1,
            grid=(NB1,),
            in_specs=[pl.BlockSpec((VB1, D), lambda v, c: (lax.rem(v + half * c[0], NB1), 0))] + [anywhere] * (len(args) - 2),
            out_specs=[pl.BlockSpec((VB1, t), lambda v, c: (v, 0)), pl.BlockSpec((1, t), lambda v, c: (0, 0)), anywhere],
            scratch_shapes=[pltpu.VMEM((t, D), BF16), pltpu.VMEM((1, t), F32), pltpu.VMEM((1, t), F32), pltpu.SemaphoreType.DMA((2, nmv))],
        ),
        out_shape=(jax.ShapeDtypeStruct((VC, t), F32), jax.ShapeDtypeStruct((1, t), F32), jax.ShapeDtypeStruct((NCH * 4 * CH, D), BF16)),
        input_output_aliases=aliases,
        compiler_params=pltpu.CompilerParams(vmem_limit_bytes=VMEM_LIMIT, dimension_semantics=("arbitrary",)),
        cost_estimate=pl.CostEstimate(flops=2 * VC * t * D, bytes_accessed=VC * t * 4 + VC * D * 2, transcendentals=VC * t),
    )(*args)


def grad_kernel(widths, outs, nskip, core_ref, w_ref, lab_ref, lse_ref, sc_ref, *refs):
    nl = len(widths)
    ls, refs = refs[:nl], refs[nl:]
    refs = refs[nskip:]
    dz_ref, pk_ref, dxs = refs[0], refs[1], refs[2:]
    v = pl.program_id(0)

    @pl.when(v == 0)
    def _():
        pk_ref[...] = jnp.zeros_like(pk_ref)
        for dx_ref in dxs:
            dx_ref[...] = jnp.zeros_like(dx_ref)

    col = 0
    for l_ref, width in zip(ls, widths):
        cols = pl.ds(col, width)
        lab = lab_ref[:, cols] - v * VB2
        lse, sc = lse_ref[:, cols], sc_ref[:, cols]
        pk = pk_ref[:, cols]
        for q in range(0, VB2, SUB):
            size = min(SUB, VB2 - q)
            rows = pl.ds(q, size)
            l = l_ref[rows, :]
            hit = lax.broadcasted_iota(jnp.int32, (size, width), 0) == lab - q
            e = jnp.exp(l - lse)
            pk = pk + jnp.sum(jnp.where(hit, l, 0.0), axis=0, keepdims=True)
            dz_ref[rows, cols] = (jnp.where(hit, e - 1.0, e) * sc).astype(BF16)
        pk_ref[:, cols] = pk
        col += width
    dx = lax.dot_general(dz_ref[...], w_ref[...], (((0,), (0,)), ((), ())), preferred_element_type=F32)
    for dx_ref, pieces in zip(dxs, outs):
        for src, dst, n in pieces:
            dx_ref[pl.ds(dst, n), :] += dx[src:src + n]


def local_grads(core, w, lab, lse, sc, ls, dz_all, slot, outs, deps):
    t = sum(width for _, width, _ in ls)
    half = NB2 // 2
    row = pl.BlockSpec((1, t), lambda v, c: (0, 0))
    in_specs = [pl.BlockSpec((VB2, D), lambda v, c: (lax.rem(v + half * c[0], NB2), 0)), row, row, row]
    in_specs += [pl.BlockSpec((VB2, width), lambda v, c, b=block: (v, b)) for _, width, block in ls]
    args = [core, w, lab, lse, sc] + [a for a, _, _ in ls] + list(deps)
    aliases = {}
    if dz_all is not None:
        aliases = {len(args): 0}
        args.append(dz_all)
    extra = len(args) - 1 - len(in_specs)
    in_specs += [pl.BlockSpec(memory_space=pl.ANY)] * extra
    heights = [sum(n for _, _, n in pieces) for pieces in outs]
    return pl.pallas_call(
        functools.partial(grad_kernel, tuple(width for _, width, _ in ls), outs, extra),
        grid_spec=pltpu.PrefetchScalarGridSpec(
            num_scalar_prefetch=1,
            grid=(NB2,),
            in_specs=in_specs,
            out_specs=[pl.BlockSpec((VB2, t), lambda v, c: (v, slot)), row] + [pl.BlockSpec((n, D), lambda v, c: (0, 0)) for n in heights],
        ),
        out_shape=[jax.ShapeDtypeStruct((VC, NCH * 4 * CH), BF16), jax.ShapeDtypeStruct((1, t), F32)]
        + [jax.ShapeDtypeStruct((n, D), F32) for n in heights],
        input_output_aliases=aliases,
        compiler_params=pltpu.CompilerParams(vmem_limit_bytes=VMEM_LIMIT, dimension_semantics=("arbitrary",)),
        cost_estimate=pl.CostEstimate(flops=2 * VC * t * D, bytes_accessed=VC * t * 6 + VC * D * 2, transcendentals=VC * t),
    )(*args)


def hop(a, bit):
    return lax.ppermute(a, AX, [(d, d ^ bit) for d in range(NDEV)])


OWN, XN, YN, DG = 0, 1, 2, 3
ORDER = [(XN, 0), (YN, 1), (DG, 0), (DG, 1), (YN, 0), (XN, 1), (OWN, 0), (OWN, 1)]
POS = {rs: i for i, rs in enumerate(ORDER)}


def in_order(a):
    h = a.reshape(4, 2, HF)
    return jnp.concatenate([h[r, s] for r, s in ORDER])[None]


def by_owner(cols):
    h = cols.reshape(8, HF)
    return jnp.stack([h[POS[r, s]] for r in range(4) for s in range(2)]).reshape(4, CH)


def after(a, *deps):
    return lax.optimization_barrier((a, *deps))[0]


def solution(mesh):
    def local_step(hidden, norm_gain, w_head, labels):
        nb, seq_len, _ = hidden.shape
        me = lax.axis_index(AX)
        core = lax.rem(me, 2)
        chip = me // 2

        w2 = lax.all_gather(w_head, AX, axis=0, tiled=True, axis_index_groups=[[2 * k, 2 * k + 1] for k in range(4)])
        small = jnp.concatenate([labels.reshape(-1).astype(F32), norm_gain.astype(F32)])
        small = lax.all_gather(small, AX, axis=0)
        lab_all = small[:, :nb * seq_len].astype(jnp.int32)
        gain = small[:, nb * seq_len:].reshape(1, D)
        count = jnp.sum((lab_all >= 0).astype(F32))

        h_c = hidden.reshape(NCH, CH, D)
        x_own = []
        for c in range(NCH):
            h = h_c[c].astype(F32)
            r = lax.rsqrt(jnp.mean(h * h, axis=-1, keepdims=True) + EPSILON)
            n = (h * r).astype(BF16)
            x_own.append((n.astype(F32) * gain).astype(BF16))

        core_arr = core[None].astype(jnp.int32)

        def whole(c, r, block):
            return [(0, block * CH, c * 4 * CH + POS[r, 0] * HF, CH)]

        def split(c, r, block):
            first = [(XN, 0), (YN, 1)]
            out = []
            for s in range(2):
                lead = (r, s) in first
                col = (0 if lead else CH) + ([XN, YN].index(r) if lead else [YN, XN].index(r)) * HF
                out.append((s * HF, block * CH + col, c * 4 * CH + POS[r, s] * HF, HF))
            return out

        x_x = [hop(x_own[c], 2) for c in range(3)]
        x_y = [hop(x_own[c], 4) for c in range(3)]
        l_own, lse_own, x_all = local_logits(core_arr, w2, x_own, [whole(c, OWN, c) for c in range(NCH)], None, [])
        late = after(x_own[3], lse_own)
        x_x.append(hop(late, 2))
        x_y.append(hop(late, 4))
        x_d = [hop(after(x_y[c], lse_own), 2) if c % 2 == 0 else hop(after(x_x[c], lse_own), 4) for c in range(2)]
        l_1, lse_1, x_all = local_logits(
            core_arr, w2, [x_x[0], x_y[0], x_x[1], x_y[1]],
            [split(0, XN, 0), split(0, YN, 0), split(1, XN, 2), split(1, YN, 2)], x_all, [])
        x_d.append(hop(after(x_y[2], lse_1), 2))
        l_2, lse_2, x_all = local_logits(
            core_arr, w2, [x_d[0], x_d[1], x_x[2], x_y[2]],
            [whole(0, DG, 0), whole(1, DG, 1), split(2, XN, 2), split(2, YN, 2)], x_all, [])
        x_d.append(hop(after(x_x[3], lse_2), 4))

        def full_lse(blocks):
            mine = jnp.stack([by_owner(jnp.concatenate(b)) for b in blocks], axis=1)
            parts = [mine] + [hop(mine, q << 1)[jnp.array([r ^ q for r in range(4)])] for q in (1, 2, 3)]
            stack = jnp.stack(parts)
            top = jnp.max(stack, axis=0)
            full = top + jnp.log(jnp.sum(jnp.exp(stack - top), axis=0))
            return [in_order(full[:, i]) for i in range(len(blocks))]

        def blk(a, i):
            return a[0, i * CH:(i + 1) * CH]

        owners = jnp.stack([me ^ (r << 1) for r in range(4)])
        lab_grp = lab_all[owners].reshape(4, NCH, CH)
        local = lab_grp - chip * VC
        here = (local >= 0) & (local < VC)
        row = jnp.where(here, lax.rem(local + VC - core * VD, VC), -1)
        scale = jnp.where(lab_grp >= 0, 1.0 / count, 0.0)
        lab_c = [in_order(row[:, c]) for c in range(NCH)]
        sc_c = [in_order(scale[:, c]) for c in range(NCH)]

        lse_c = full_lse([
            [blk(lse_1, 0), blk(lse_2, 0), blk(lse_1, 1), blk(lse_own, 0)],
            [blk(lse_1, 2), blk(lse_2, 1), blk(lse_1, 3), blk(lse_own, 1)]])
        t = 2 * CH
        send_outs = (((0, 0, HF), (CH, HF, HF)), ((HF, 0, HF), (CH + HF, HF, HF)))
        keep_outs = (((0, 0, HF),), ((HF, 0, HF),), ((CH, 0, CH),))
        l_xy = [(l_1, 0), (l_1, 2), (l_2, 2), None]
        l_dg = [(l_2, 0), (l_2, 1), None, None]
        dz_all, loss_sum = None, 0.0
        dx_own, arrived, pending = [], [], []

        def forward(c):
            (in_a, in_b), (k_y, k_x, k_own) = arrived[c]
            add_a, add_b = k_y + in_a[HF:], k_x + in_b[HF:]
            pending.append((hop(add_a, 4), hop(add_b, 2)))
            return [add_a, add_b]

        for c in range(NCH):
            deps_out, deps_keep = [], []
            if c == 1:
                deps_out = [lse_3] + forward(0)
            if c == 2:
                deps_out = list(pending[0])
            if c >= 2:
                deps_keep = forward(c - 1)
            (a_xy, b_xy), (a_dg, b_dg) = l_xy[c], l_dg[c]
            dz_all, pk1, send_a, send_b = local_grads(
                core_arr, w2, lab_c[c][:, :t], lse_c[c][:, :t], sc_c[c][:, :t], [(a_xy, CH, b_xy), (a_dg, CH, b_dg)], dz_all, 2 * c,
                send_outs, deps_out)
            incoming = (hop(send_a, 2), hop(send_b, 4))
            dz_all, pk2, k_y, k_x, k_own = local_grads(
                core_arr, w2, lab_c[c][:, t:], lse_c[c][:, t:], sc_c[c][:, t:], [(a_xy, CH, b_xy + 1), (l_own, CH, c)], dz_all, 2 * c + 1,
                keep_outs, deps_keep)
            arrived.append((incoming, (k_y, k_x, k_own)))
            pk = jnp.concatenate([pk1, pk2], axis=1)
            loss_sum = loss_sum + jnp.sum(jnp.where(lab_c[c] >= 0, lse_c[c] - pk, 0.0))
            if c == 0:
                l_3, lse_3, x_all = local_logits(
                    core_arr, w2, [x_d[2], x_d[3], x_x[3], x_y[3]],
                    [whole(2, DG, 0), whole(3, DG, 1), split(3, XN, 2), split(3, YN, 2)], x_all, [pk2])
                l_dg[2:] = [(l_3, 0), (l_3, 1)]
                l_xy[3] = (l_3, 2)
                lse_c += full_lse([
                    [blk(lse_2, 2), blk(lse_3, 0), blk(lse_2, 3), blk(lse_own, 2)],
                    [blk(lse_3, 2), blk(lse_3, 1), blk(lse_3, 3), blk(lse_own, 3)]])

        def dw_part(rows, cols):
            return jnp.einsum("vt,td->vd", dz_all[rows, cols], x_all[cols], preferred_element_type=F32)

        every, head, rest = slice(None), slice(0, 2 * NCH * CH), slice(2 * NCH * CH, None)
        dz_all, *pending[1] = lax.optimization_barrier((dz_all, *pending[1]))
        dw_other = dw_part(slice(VD, None), every)
        arrived[3] = after(arrived[3], dw_other[:8, :128])
        forward(NCH - 1)
        dw_other = hop(dw_other, 1)
        x_all, *pending[2] = lax.optimization_barrier((x_all, *pending[2]))
        dw_mine = dw_part(slice(0, VD), head)
        pending[3] = after(pending[3], dw_mine[:8, :128])

        for c in range(NCH):
            (in_a, in_b), (_, _, k_own) = arrived[c]
            fin_a, fin_b = pending[c]
            dx_own.append(jnp.concatenate([k_own[:HF] + in_a[:HF] + fin_a, k_own[HF:] + in_b[:HF] + fin_b]))

        dg, dh = 0.0, []
        for c in range(NCH):
            gx = dx_own[c].astype(BF16).astype(F32)
            h = h_c[c].astype(F32)
            r = lax.rsqrt(jnp.mean(h * h, axis=-1, keepdims=True) + EPSILON)
            n = (h * r).astype(BF16).astype(F32)
            dg = dg + jnp.sum(gx * n, axis=0)
            gn = gx * gain
            proj = jnp.mean(gn * h, axis=-1, keepdims=True)
            dh.append((r * gn - h * r ** 3 * proj).astype(BF16))
        dz_all, dg = lax.optimization_barrier((dz_all, dg))
        grad_w = dw_part(slice(0, VD), rest) + (dw_mine + dw_other)
        tail = lax.psum(jnp.concatenate([dg, jnp.full((128,), loss_sum, F32)]), AX)
        grad_g = lax.dynamic_slice(tail, (me * (D // NDEV),), (D // NDEV,))
        loss_value = tail[D] / count
        return loss_value, jnp.concatenate(dh).reshape(nb, seq_len, D), grad_w, grad_g

    return jax.shard_map(local_step, mesh=mesh, in_specs=(P(AX, None, None), P(AX), P(AX, None), P(AX, None)), out_specs=(P(), P(AX, None, None), P(AX, None), P(AX)), check_vma=False)
```

time: 2840 us -> 1470 us (0.52)
  waiting for transfers between devices: 1630 us -> 146 us
  Pallas kernels: 0 us -> 790 us
  matrix products: 873 us -> 305 us
  other arithmetic: 245 us -> 96.3 us
  starting transfers between devices: 0.08 us -> 36.6 us
    unnamed x3 -> x1, waiting for transfers between devices: 1090 us -> 0.68 us
    pallas_call x0 -> x12, Pallas kernels: none -> 790 us  [the longest x8 423 us: local_grads(): pl.pallas_call(functools.partial(grad_kernel, tuple((width for _, width,...]
    dot_general x3, matrix products: 873 us -> 305 us  [dw_part(): jnp.einsum('vt,td->vd', dz_all[rows, cols], x_all[cols], preferred_elemen...]
    all_gather x1, waiting for transfers between devices: 544 us -> 5.9 us  [local_step(): lax.all_gather(w_head, AX, axis=0, tiled=True, axis_index_groups=[[2 * k,...]
    ppermute x0 -> x35, waiting for transfers between devices: none -> 139 us  [hop(): return lax.ppermute(a, AX, [(d, d ^ bit) for d in range(NDEV)])]
    convert_element_type x4 -> x3, other arithmetic: 144 us -> 13.1 us  [the longest x1 7.26 us: local_step(): dh.append((r * gn - h * r ** 3 * proj).astype(BF16))]
    reduce_sum x3 -> x10, other arithmetic: 99.8 us -> 23.4 us  [the longest x2 12.5 us: local_step(): proj = jnp.mean(gn * h, axis=-1, keepdims=True)]
    ppermute x0 -> x35, starting transfers between devices: none -> 36.6 us  [hop(): return lax.ppermute(a, AX, [(d, d ^ bit) for d in range(NDEV)])]
  transfers between devices with their start and end apart: 2 -> 36, of which waited for: 2 -> 6; matrix products, arithmetic and copies ran while one was open for 11% -> 13% of each run, Pallas kernels for 0% -> 54%
where the time goes in v1:
time: 1470 us; the launch traced here: 1460 us
  Pallas kernels  790 us (54%)
  matrix products  305 us (21%)
  waiting for transfers between devices  146 us (10%)
  other arithmetic  96.3 us (7%)
  starting transfers between devices  36.6 us (2%)
  blocking collectives  36.6 us (2%)
  local copies, waits for them, and re-layouts  25 us (2%)
  between operations  22.6 us (2%)
    pallas_call x8, Pallas kernels, local_grads(): pl.pallas_call(functools.partial(grad_kernel, tuple((width for _, width,...  423 us
    pallas_call x4, Pallas kernels, local_logits(): pl.pallas_call(functools.partial(logits_kernel, moves, x_all is not None,...  368 us
    dot_general x3, matrix products, dw_part(): jnp.einsum('vt,td->vd', dz_all[rows, cols], x_all[cols], preferred_elemen...  305 us
    ppermute x35, waiting for transfers between devices, hop(): return lax.ppermute(a, AX, [(d, d ^ bit) for d in range(NDEV)])  139 us
    ppermute x35, starting transfers between devices, hop(): return lax.ppermute(a, AX, [(d, d ^ bit) for d in range(NDEV)])  36.6 us
  transfers between devices with their start and end apart: 36, of which 6 were waited for; matrix products, arithmetic and copies ran while one was open for 13% of the time, Pallas kernels for 54%

profile of v1, /device:TPU:0, one launch (start us, length us, event | category | flops | bytes accessed | tf_op | source)
XLA Modules:
  0.0 1458.3 jit_solution(7836644552456150803)
XLA Ops:
  8.0 13.9 all-gather.1
  21.9 7.6 fusion.42
  30.7 2.7 copy-done
  33.4 5.8 fusion.25
  39.6 1.5 collective-permute-start.2
  41.7 1.7 collective-permute-start
  53.7 5.9 all-gather.4.cloned.1.call-done.w_ref
  59.6 88.7 %shard_map.129 = (f32[8000,2048]{1,0:T(8,128)}, f32[1,2048]{1,0:T(1,128)}, bf16[8192,2048]{1,0:T(8,128)(2,1)}) custom-call(s32[1]{0:T(128)} %bitcast.core_ref, bf16[8000,2048]{1,0:T(8,128)(2,1)} %all-gather.4.cloned.1.call-done.w_ref, bf16[512,2048]{1,0:T(8,128)(2,1)} %get-tuple-element.175.refs_0_, bf16[512,2048]{1,0:T(8,128)(2,1)} %get-tuple-element.173.refs_1_, ...), custom_call_target="tpu_custom_call" | custom-call | flops 67108864000 | bytes 98304000 | tf_op jit(solution)/shard_map/pallas_call | solution.py:79
  148.3 1.8 collective-permute-start.4
  150.4 1.7 collective-permute-start.1
  153.6 101.2 %shard_map.130 = (f32[8000,2048]{1,0:T(8,128)}, f32[1,2048]{1,0:T(1,128)}, bf16[8192,2048]{1,0:T(8,128)(2,1)}) custom-call(s32[1]{0:T(128)} %bitcast.core_ref, bf16[8000,2048]{1,0:T(8,128)(2,1)} %all-gather.4.cloned.1.call-done.w_ref, bf16[512,2048]{1,0:T(8,128)(2,1)} %collective-permute-done.6.refs_0_, ...), custom_call_target="tpu_custom_call", output_to_operand_aliasing={{2}: (6, {})} | custom-call | flops 67108864000 | bytes 98304000 | tf_op jit(solution)/shard_map/pallas_call | solution.py:79
  256.2 30.2 %collective-permute-done.1.refs_0_ = bf16[512,2048]{1,0:T(8,128)(2,1)} collective-permute-done((bf16[512,2048]{1,0:T(8,128)(2,1)}, bf16[512,2048]{1,0:T(8,128)(2,1)}, u32[]{:S(2)}, u32[]{:S(2)}) %collective-permute-start.1) | collective-permute-done | bytes 2097184 | tf_op jit(solution)/shard_map/ppermute | solution.py:161
  286.4 88.8 %shard_map.131 = (f32[8000,2048]{1,0:T(8,128)}, f32[1,2048]{1,0:T(1,128)}, bf16[8192,2048]{1,0:T(8,128)(2,1)}) custom-call(s32[1]{0:T(128)} %bitcast.core_ref, bf16[8000,2048]{1,0:T(8,128)(2,1)} %all-gather.4.cloned.1.call-done.w_ref, bf16[512,2048]{1,0:T(8,128)(2,1)} %collective-permute-done.1.refs_0_, ...), custom_call_target="tpu_custom_call", output_to_operand_aliasing={{2}: (6, {})} | custom-call | flops 67108864000 | bytes 98304000 | tf_op jit(solution)/shard_map/pallas_call | solution.py:79
  376.7 1.8 collective-permute-start.13
  380.2 1.8 collective-permute-start.11
  387.8 52.8 %shard_map.132 = (bf16[8000,8192]{1,0:T(8,128)(2,1)}, f32[1,1024]{1,0:T(1,128)}, f32[512,2048]{1,0:T(8,128)}, f32[512,2048]{1,0:T(8,128)}) custom-call(s32[1]{0:T(128)} %bitcast.core_ref, bf16[8000,2048]{1,0:T(8,128)(2,1)} %all-gather.4.cloned.1.call-done.w_ref, s32[1,1024]{1,0:T(1,128)} %get-tuple-element.300.lab_ref, ...), custom_call_target="tpu_custom_call" | custom-call | flops 33554432000 | bytes 81920000 | tf_op jit(solution)/shard_map/pallas_call | solution.py:144
  440.9 1.7 collective-permute-start.19
  442.7 53.0 %shard_map.133 = (bf16[8000,8192]{1,0:T(8,128)(2,1)}, f32[1,1024]{1,0:T(1,128)}, f32[256,2048]{1,0:T(8,128)}, f32[256,2048]{1,0:T(8,128)}, f32[512,2048]{1,0:T(8,128)}) custom-call(s32[1]{0:T(128)} %bitcast.core_ref, bf16[8000,2048]{1,0:T(8,128)(2,1)} %all-gather.4.cloned.1.call-done.w_ref, ...), custom_call_target="tpu_custom_call", output_to_operand_aliasing={{0}: (7, {})} | custom-call | flops 33554432000 | bytes 81920000 | tf_op jit(solution)/shard_map/pallas_call | solution.py:144
  495.8 88.9 %shard_map.134 = (f32[8000,2048]{1,0:T(8,128)}, f32[1,2048]{1,0:T(1,128)}, bf16[8192,2048]{1,0:T(8,128)(2,1)}) custom-call(s32[1]{0:T(128)} %bitcast.core_ref, bf16[8000,2048]{1,0:T(8,128)(2,1)} %all-gather.4.cloned.1.call-done.w_ref, bf16[512,2048]{1,0:T(8,128)(2,1)} %collective-permute-done.8.refs_0_, ...), custom_call_target="tpu_custom_call", output_to_operand_aliasing={{2}: (7, {})} | custom-call | flops 67108864000 | bytes 98304000 | tf_op jit(solution)/shard_map/pallas_call | solution.py:79
  586.0 2.6 collective-permute-start.17
  594.8 3.9 slice_add_fusion.10.refs_4_
  599.6 3.2 slice_add_fusion.11.refs_3_
  604.1 52.7 %shard_map.135 = (bf16[8000,8192]{1,0:T(8,128)(2,1)}, f32[1,1024]{1,0:T(1,128)}, f32[512,2048]{1,0:T(8,128)}, f32[512,2048]{1,0:T(8,128)}) custom-call(s32[1]{0:T(128)} %bitcast.core_ref, bf16[8000,2048]{1,0:T(8,128)(2,1)} %all-gather.4.cloned.1.call-done.w_ref, s32[1,1024]{1,0:T(1,128)} %get-tuple-element.206.lab_ref, ...), custom_call_target="tpu_custom_call", output_to_operand_aliasing={{0}: (10, {})} | custom-call | flops 33554432000 | bytes 81920000 | tf_op jit(solution)/shard_map/pallas_call | solution.py:144
  658.8 52.8 %shard_map.136 = (bf16[8000,8192]{1,0:T(8,128)(2,1)}, f32[1,1024]{1,0:T(1,128)}, f32[256,2048]{1,0:T(8,128)}, f32[256,2048]{1,0:T(8,128)}, f32[512,2048]{1,0:T(8,128)}) custom-call(s32[1]{0:T(128)} %bitcast.core_ref, bf16[8000,2048]{1,0:T(8,128)(2,1)} %all-gather.4.cloned.1.call-done.w_ref, ...), custom_call_target="tpu_custom_call", output_to_operand_aliasing={{0}: (7, {})} | custom-call | flops 33554432000 | bytes 81920000 | tf_op jit(solution)/shard_map/pallas_call | solution.py:144
  711.6 52.8 %shard_map.137 = (bf16[8000,8192]{1,0:T(8,128)(2,1)}, f32[1,1024]{1,0:T(1,128)}, f32[512,2048]{1,0:T(8,128)}, f32[512,2048]{1,0:T(8,128)}) custom-call(s32[1]{0:T(128)} %bitcast.core_ref, bf16[8000,2048]{1,0:T(8,128)(2,1)} %all-gather.4.cloned.1.call-done.w_ref, s32[1,1024]{1,0:T(1,128)} %get-tuple-element.200.lab_ref, ...), custom_call_target="tpu_custom_call", output_to_operand_aliasing={{0}: (9, {})} | custom-call | flops 33554432000 | bytes 81920000 | tf_op jit(solution)/shard_map/pallas_call | solution.py:144
  766.6 3.9 slice_add_fusion.9.refs_2_
  771.3 3.2 slice_add_fusion.8.refs_3_
  775.6 52.9 %shard_map.138 = (bf16[8000,8192]{1,0:T(8,128)(2,1)}, f32[1,1024]{1,0:T(1,128)}, f32[256,2048]{1,0:T(8,128)}, f32[256,2048]{1,0:T(8,128)}, f32[512,2048]{1,0:T(8,128)}) custom-call(s32[1]{0:T(128)} %bitcast.core_ref, bf16[8000,2048]{1,0:T(8,128)(2,1)} %all-gather.4.cloned.1.call-done.w_ref, ...), custom_call_target="tpu_custom_call", output_to_operand_aliasing={{0}: (9, {})} | custom-call | flops 33554432000 | bytes 81920000 | tf_op jit(solution)/shard_map/pallas_call | solution.py:144
  828.5 53.1 %shard_map.139 = (bf16[8000,8192]{1,0:T(8,128)(2,1)}, f32[1,1024]{1,0:T(1,128)}, f32[512,2048]{1,0:T(8,128)}, f32[512,2048]{1,0:T(8,128)}) custom-call(s32[1]{0:T(128)} %bitcast.core_ref, bf16[8000,2048]{1,0:T(8,128)(2,1)} %all-gather.4.cloned.1.call-done.w_ref, s32[1,1024]{1,0:T(1,128)} %get-tuple-element.194.lab_ref, ...), custom_call_target="tpu_custom_call", output_to_operand_aliasing={{0}: (7, {})} | custom-call | flops 33554432000 | bytes 81920000 | tf_op jit(solution)/shard_map/pallas_call | solution.py:144
  881.7 4.0 slice_add_fusion.7.refs_2_
  885.7 3.2 slice_add_fusion.6.refs_3_
  888.9 52.6 %shard_map.140 = (bf16[8000,8192]{1,0:T(8,128)(2,1)}, f32[1,1024]{1,0:T(1,128)}, f32[256,2048]{1,0:T(8,128)}, f32[256,2048]{1,0:T(8,128)}, f32[512,2048]{1,0:T(8,128)}) custom-call(s32[1]{0:T(128)} %bitcast.core_ref, bf16[8000,2048]{1,0:T(8,128)(2,1)} %all-gather.4.cloned.1.call-done.w_ref, ...), custom_call_target="tpu_custom_call", output_to_operand_aliasing={{0}: (9, {})} | custom-call | flops 33554432000 | bytes 81920000 | tf_op jit(solution)/shard_map/pallas_call | solution.py:144
  941.7 148.2 %fusion = f32[4000,2048]{1,0:T(8,128)} fusion(bf16[8192,2048]{1,0:T(8,128)(2,1)} %get-tuple-element.139, bf16[8000,8192]{1,0:T(8,128)(2,1)} %get-tuple-element.138), kind=kOutput, calls=%fused_computation.7 | convolution fusion | flops 134217728000 | bytes 131858432 | tf_op jit(solution)/shard_map/vt,td->vd/dot_general | solution.py:302
  1096.4 7.2 fusion.57
  1108.1 7.2 fusion.53
  1115.3 70.5 %collective-permute-done.30 = f32[512,2048]{1,0:T(8,128)} collective-permute-done((f32[512,2048]{1,0:T(8,128)}, f32[512,2048]{1,0:T(8,128)}, u32[]{:S(2)}, u32[]{:S(2)}) %collective-permute-start.30) | collective-permute-done | bytes 4194336 | tf_op jit(solution)/shard_map/ppermute | solution.py:161
  1186.8 3.2 slice_add_fusion.12
  1191.1 3.3 slice_add_fusion.13
  1195.1 36.7 %collective-permute-done.28 = f32[256,2048]{1,0:T(8,128)} collective-permute-done((f32[256,2048]{1,0:T(8,128)S(1)}, f32[256,2048]{1,0:T(8,128)}, u32[]{:S(2)}, u32[]{:S(2)}) %collective-permute-start.28) | collective-permute-done | bytes 2097184 | tf_op jit(solution)/shard_map/ppermute | solution.py:161
  1231.8 76.9 %fusion.2 = f32[4000,2048]{1,0:T(8,128)} fusion(bf16[8000,8192]{1,0:T(8,128)(2,1)} %get-tuple-element.138, bf16[8192,2048]{1,0:T(8,128)(2,1)} %get-tuple-element.139), kind=kOutput, calls=%fused_computation.10 | convolution fusion | flops 67108864000 | bytes 82313216 | tf_op jit(solution)/shard_map/vt,td->vd/dot_general | solution.py:302
  1308.7 5.9 fusion.49
  1314.7 5.4 add_convert_fusion.1
  1320.4 5.9 fusion.41
  1326.4 6.6 fusion.33
  1333.0 22.7 %psum.7 = f32[2176]{0:T(1024)S(1)} all-reduce(f32[2176]{0:T(1024)S(1)} %concatenate.425), channel_id=1, replica_groups=mesh['fsdp'=8] {'fsdp'}, use_global_device_ids=true, to_apply=%region_15.16 | all-reduce | flops 2176 | bytes 17408 | tf_op jit(solution)/shard_map/psum | solution.py:331
  1358.3 7.3 fusion.21
  1365.6 4.0 pad_maximum_fusion
  1369.5 80.3 %add_add_fusion = f32[4000,2048]{1,0:T(8,128)} fusion(f32[4000,2048]{1,0:T(8,128)} %fusion.2, f32[4000,2048]{1,0:T(8,128)} %collective-permute-done.34, bf16[8000,8192]{1,0:T(8,128)(2,1)} %get-tuple-element.138, bf16[8192,2048]{1,0:T(8,128)(2,1)} %get-tuple-element.139), kind=kOutput, calls=%fused_computation.9 | convolution fusion | flops 67125248000 | bytes 147849216 | tf_op jit(solution)/shard_map/vt,td->vd/dot_general | solution.py:302
  (477 shorter events, 51.9 us)
Async XLA Ops:
  7.2 52.4 %all-gather.4.cloned.1.call-start = ((), (), s32[]{:S(2)}) async-start(), calls=%async_computation | async-start | bytes 49152000 | tf_op jit(solution)/shard_map/all_gather | solution.py:190
  39.3 111.1 %collective-permute-start.7 = (bf16[512,2048]{1,0:T(8,128)(2,1)}, bf16[512,2048]{1,0:T(8,128)(2,1)}, u32[]{:S(2)}, u32[]{:S(2)}) collective-permute-start(bf16[512,2048]{1,0:T(8,128)(2,1)} %get-tuple-element.173.refs_1_), channel_id=1, source_target_pairs={{0,4},{1,5},{2,6},{3,7},{4,0},{5,1},{6,2},{7,3}} | collective-permute-start | bytes 6291464 | tf_op jit(solution)/shard_map/ppermute | solution.py:161
  39.6 108.7 %collective-permute-start.2 = (bf16[512,2048]{1,0:T(8,128)(2,1)}, bf16[512,2048]{1,0:T(8,128)(2,1)}, u32[]{:S(2)}, u32[]{:S(2)}) collective-permute-start(bf16[512,2048]{1,0:T(8,128)(2,1)} %get-tuple-element.173.refs_1_), channel_id=1, source_target_pairs={{0,2},{1,3},{2,0},{3,1},{4,6},{5,7},{6,4},{7,5}} | collective-permute-start | bytes 6291464 | tf_op jit(solution)/shard_map/ppermute | solution.py:161
  41.1 111.0 %collective-permute-start.6 = (bf16[512,2048]{1,0:T(8,128)(2,1)}, bf16[512,2048]{1,0:T(8,128)(2,1)}, u32[]{:S(2)}, u32[]{:S(2)}) collective-permute-start(bf16[512,2048]{1,0:T(8,128)(2,1)} %get-tuple-element.175.refs_0_), channel_id=1, source_target_pairs={{0,2},{1,3},{2,0},{3,1},{4,6},{5,7},{6,4},{7,5}} | collective-permute-start | bytes 6291464 | tf_op jit(solution)/shard_map/ppermute | solution.py:161
  41.7 108.4 %collective-permute-start = (bf16[512,2048]{1,0:T(8,128)(2,1)}, bf16[512,2048]{1,0:T(8,128)(2,1)}, u32[]{:S(2)}, u32[]{:S(2)}) collective-permute-start(bf16[512,2048]{1,0:T(8,128)(2,1)} %get-tuple-element.175.refs_0_), channel_id=1, source_target_pairs={{0,4},{1,5},{2,6},{3,7},{4,0},{5,1},{6,2},{7,3}} | collective-permute-start | bytes 6291464 | tf_op jit(solution)/shard_map/ppermute | solution.py:161
  43.4 212.9 %collective-permute-start.5 = (bf16[512,2048]{1,0:T(8,128)(2,1)}, bf16[512,2048]{1,0:T(8,128)(2,1)}, u32[]{:S(2)}, u32[]{:S(2)}) collective-permute-start(bf16[512,2048]{1,0:T(8,128)(2,1)} %get-tuple-element.174.refs_2_), channel_id=1, source_target_pairs={{0,4},{1,5},{2,6},{3,7},{4,0},{5,1},{6,2},{7,3}} | collective-permute-start | bytes 6291464 | tf_op jit(solution)/shard_map/ppermute | solution.py:161
  148.3 107.9 %collective-permute-start.4 = (bf16[512,2048]{1,0:T(8,128)(2,1)}, bf16[512,2048]{1,0:T(8,128)(2,1)}, u32[]{:S(2)}, u32[]{:S(2)}) collective-permute-start(bf16[512,2048]{1,0:T(8,128)(2,1)} %get-tuple-element.174.refs_2_), channel_id=1, source_target_pairs={{0,2},{1,3},{2,0},{3,1},{4,6},{5,7},{6,4},{7,5}} | collective-permute-start | bytes 6291464 | tf_op jit(solution)/shard_map/ppermute | solution.py:161
  150.1 231.9 %collective-permute-start.9 = (bf16[512,2048]{1,0:T(8,128)(2,1)}, bf16[512,2048]{1,0:T(8,128)(2,1)}, u32[]{:S(2)}, u32[]{:S(2)}) collective-permute-start(bf16[512,2048]{1,0:T(8,128)(2,1)} %get-tuple-element.80.refs_3_), channel_id=1, source_target_pairs={{0,2},{1,3},{2,0},{3,1},{4,6},{5,7},{6,4},{7,5}} | collective-permute-start | bytes 6291464 | tf_op jit(solution)/shard_map/ppermute | solution.py:161
  150.4 136.0 %collective-permute-start.1 = (bf16[512,2048]{1,0:T(8,128)(2,1)}, bf16[512,2048]{1,0:T(8,128)(2,1)}, u32[]{:S(2)}, u32[]{:S(2)}) collective-permute-start(bf16[512,2048]{1,0:T(8,128)(2,1)} %collective-permute-done.refs_1_), channel_id=1, source_target_pairs={{0,2},{1,3},{2,0},{3,1},{4,6},{5,7},{6,4},{7,5}} | collective-permute-start | bytes 6291464 | tf_op jit(solution)/shard_map/ppermute | solution.py:161
  152.1 134.2 %collective-permute-start.3 = (bf16[512,2048]{1,0:T(8,128)(2,1)}, bf16[512,2048]{1,0:T(8,128)(2,1)}, u32[]{:S(2)}, u32[]{:S(2)}) collective-permute-start(bf16[512,2048]{1,0:T(8,128)(2,1)} %collective-permute-done.2.refs_2_), channel_id=1, source_target_pairs={{0,4},{1,5},{2,6},{3,7},{4,0},{5,1},{6,2},{7,3}} | collective-permute-start | bytes 6291464 | tf_op jit(solution)/shard_map/ppermute | solution.py:161
  153.6 101.2 %copy-start.46 = (f32[1,2048]{1,0:T(1,128)S(1)}, f32[1,2048]{1,0:T(1,128)}, u32[]{:S(2)}) copy-start(f32[1,2048]{1,0:T(1,128)} %get-tuple-element.72) | copy-start | bytes 24580
  376.7 6.8 collective-permute-start.13
  378.4 6.3 collective-permute-start.14
  379.9 5.6 collective-permute-start.12
  380.2 115.4 %collective-permute-start.11 = (bf16[512,2048]{1,0:T(8,128)(2,1)}, bf16[512,2048]{1,0:T(8,128)(2,1)}, u32[]{:S(2)}, u32[]{:S(2)}) collective-permute-start(bf16[512,2048]{1,0:T(8,128)(2,1)} %get-tuple-element.80.refs_3_), channel_id=1, source_target_pairs={{0,4},{1,5},{2,6},{3,7},{4,0},{5,1},{6,2},{7,3}} | collective-permute-start | bytes 6291464 | tf_op jit(solution)/shard_map/ppermute | solution.py:161
  382.0 113.6 %collective-permute-start.8 = (bf16[512,2048]{1,0:T(8,128)(2,1)}, bf16[512,2048]{1,0:T(8,128)(2,1)}, u32[]{:S(2)}, u32[]{:S(2)}) collective-permute-start(bf16[512,2048]{1,0:T(8,128)(2,1)} %collective-permute-done.5.refs_3_), channel_id=1, source_target_pairs={{0,2},{1,3},{2,0},{3,1},{4,6},{5,7},{6,4},{7,5}} | collective-permute-start | bytes 6291464 | tf_op jit(solution)/shard_map/ppermute | solution.py:161
  383.5 112.2 %collective-permute-start.10 = (bf16[512,2048]{1,0:T(8,128)(2,1)}, bf16[512,2048]{1,0:T(8,128)(2,1)}, u32[]{:S(2)}, u32[]{:S(2)}) collective-permute-start(bf16[512,2048]{1,0:T(8,128)(2,1)} %collective-permute-done.9.refs_2_), channel_id=1, source_target_pairs={{0,4},{1,5},{2,6},{3,7},{4,0},{5,1},{6,2},{7,3}} | collective-permute-start | bytes 6291464 | tf_op jit(solution)/shard_map/ppermute | solution.py:161
  440.6 159.0 %collective-permute-start.18 = (f32[512,2048]{1,0:T(8,128)}, f32[512,2048]{1,0:T(8,128)}, u32[]{:S(2)}, u32[]{:S(2)}) collective-permute-start(f32[512,2048]{1,0:T(8,128)} %get-tuple-element.91), channel_id=1, source_target_pairs={{0,2},{1,3},{2,0},{3,1},{4,6},{5,7},{6,4},{7,5}} | collective-permute-start | bytes 12582920 | tf_op jit(solution)/shard_map/ppermute | solution.py:161
  440.9 153.9 %collective-permute-start.19 = (f32[512,2048]{1,0:T(8,128)}, f32[512,2048]{1,0:T(8,128)}, u32[]{:S(2)}, u32[]{:S(2)}) collective-permute-start(f32[512,2048]{1,0:T(8,128)} %get-tuple-element.93), channel_id=1, source_target_pairs={{0,4},{1,5},{2,6},{3,7},{4,0},{5,1},{6,2},{7,3}} | collective-permute-start | bytes 12582920 | tf_op jit(solution)/shard_map/ppermute | solution.py:161
  495.8 97.7 %copy-start.44 = (f32[2048]{0:T(1024)S(1)}, f32[2048]{0:T(1024)}, u32[]{:S(2)}) copy-start(f32[2048]{0:T(1024)} %custom-call.12) | copy-start | bytes 24580
  585.7 4.7 collective-permute-start.16
  586.0 5.1 collective-permute-start.17
  588.6 3.7 collective-permute-start.15
  598.7 112.9 %collective-permute-start.23 = (f32[256,2048]{1,0:T(8,128)}, f32[256,2048]{1,0:T(8,128)}, u32[]{:S(2)}, u32[]{:S(2)}) collective-permute-start(f32[256,2048]{1,0:T(8,128)} %slice_add_fusion.10.refs_4_), channel_id=1, source_target_pairs={{0,2},{1,3},{2,0},{3,1},{4,6},{5,7},{6,4},{7,5}} | collective-permute-start | bytes 6291464 | tf_op jit(solution)/shard_map/ppermute | solution.py:161
  602.9 108.7 %collective-permute-start.22 = (f32[256,2048]{1,0:T(8,128)}, f32[256,2048]{1,0:T(8,128)}, u32[]{:S(2)}, u32[]{:S(2)}) collective-permute-start(f32[256,2048]{1,0:T(8,128)} %slice_add_fusion.11.refs_3_), channel_id=1, source_target_pairs={{0,4},{1,5},{2,6},{3,7},{4,0},{5,1},{6,2},{7,3}} | collective-permute-start | bytes 6291464 | tf_op jit(solution)/shard_map/ppermute | solution.py:161
  656.9 109.7 %collective-permute-start.20 = (f32[512,2048]{1,0:T(8,128)}, f32[512,2048]{1,0:T(8,128)}, u32[]{:S(2)}, u32[]{:S(2)}) collective-permute-start(f32[512,2048]{1,0:T(8,128)} %get-tuple-element.97), channel_id=1, source_target_pairs={{0,2},{1,3},{2,0},{3,1},{4,6},{5,7},{6,4},{7,5}} | collective-permute-start | bytes 12582920 | tf_op jit(solution)/shard_map/ppermute | solution.py:161
  657.4 113.8 %collective-permute-start.21 = (f32[512,2048]{1,0:T(8,128)}, f32[512,2048]{1,0:T(8,128)}, u32[]{:S(2)}, u32[]{:S(2)}) collective-permute-start(f32[512,2048]{1,0:T(8,128)} %get-tuple-element.99), channel_id=1, source_target_pairs={{0,4},{1,5},{2,6},{3,7},{4,0},{5,1},{6,2},{7,3}} | collective-permute-start | bytes 12582920 | tf_op jit(solution)/shard_map/ppermute | solution.py:161
  764.4 117.3 %collective-permute-start.24 = (f32[512,2048]{1,0:T(8,128)}, f32[512,2048]{1,0:T(8,128)}, u32[]{:S(2)}, u32[]{:S(2)}) collective-permute-start(f32[512,2048]{1,0:T(8,128)} %get-tuple-element.103), channel_id=1, source_target_pairs={{0,2},{1,3},{2,0},{3,1},{4,6},{5,7},{6,4},{7,5}} | collective-permute-start | bytes 12582920 | tf_op jit(solution)/shard_map/ppermute | solution.py:161
  765.3 120.4 %collective-permute-start.25 = (f32[512,2048]{1,0:T(8,128)}, f32[512,2048]{1,0:T(8,128)}, u32[]{:S(2)}, u32[]{:S(2)}) collective-permute-start(f32[512,2048]{1,0:T(8,128)} %get-tuple-element.105), channel_id=1, source_target_pairs={{0,4},{1,5},{2,6},{3,7},{4,0},{5,1},{6,2},{7,3}} | collective-permute-start | bytes 12582920 | tf_op jit(solution)/shard_map/ppermute | solution.py:161
  770.5 171.1 %collective-permute-start.26 = (f32[256,2048]{1,0:T(8,128)}, f32[256,2048]{1,0:T(8,128)}, u32[]{:S(2)}, u32[]{:S(2)}) collective-permute-start(f32[256,2048]{1,0:T(8,128)} %slice_add_fusion.9.refs_2_), channel_id=1, source_target_pairs={{0,4},{1,5},{2,6},{3,7},{4,0},{5,1},{6,2},{7,3}} | collective-permute-start | bytes 6291464 | tf_op jit(solution)/shard_map/ppermute | solution.py:161
  774.5 167.1 %collective-permute-start.27 = (f32[256,2048]{1,0:T(8,128)}, f32[256,2048]{1,0:T(8,128)}, u32[]{:S(2)}, u32[]{:S(2)}) collective-permute-start(f32[256,2048]{1,0:T(8,128)} %slice_add_fusion.8.refs_3_), channel_id=1, source_target_pairs={{0,2},{1,3},{2,0},{3,1},{4,6},{5,7},{6,4},{7,5}} | collective-permute-start | bytes 6291464 | tf_op jit(solution)/shard_map/ppermute | solution.py:161
  941.6 148.3 %copy-start.39 = (f32[1,2048]{1,0:T(1,128)S(1)}, f32[1,2048]{1,0:T(1,128)}, u32[]{:S(2)}) copy-start(f32[1,2048]{1,0:T(1,128)} %constant_dynamic-update-slice_fusion.22) | copy-start | bytes 24580
  941.6 149.7 %copy-start.37 = (s32[1,2048]{1,0:T(1,128)S(1)}, s32[1,2048]{1,0:T(1,128)}, u32[]{:S(2)}) copy-start(s32[1,2048]{1,0:T(1,128)} %copy-done.36) | copy-start | bytes 24580
  941.6 149.7 %copy-start.51 = (f32[1,1024]{1,0:T(1,128)S(1)}, f32[1,1024]{1,0:T(1,128)}, u32[]{:S(2)}) copy-start(f32[1,1024]{1,0:T(1,128)} %get-tuple-element.131) | copy-start | bytes 12292
  941.6 149.7 %copy-start.52 = (f32[1,1024]{1,0:T(1,128)S(1)}, f32[1,1024]{1,0:T(1,128)}, u32[]{:S(2)}) copy-start(f32[1,1024]{1,0:T(1,128)} %get-tuple-element.86.refs_4_) | copy-start | bytes 12292
  941.6 150.3 %copy-start.18 = (f32[4,2,256]{2,1,0:T(2,128)S(1)}, f32[4,2,256]{2,1,0:T(2,128)}, u32[]{:S(2)}) copy-start(f32[4,2,256]{2,1,0:T(2,128)} %copy-done.17) | copy-start | bytes 24580
  941.6 150.4 %copy-start.23 = (f32[4,2,256]{2,1,0:T(2,128)S(1)}, f32[4,2,256]{2,1,0:T(2,128)}, u32[]{:S(2)}) copy-start(f32[4,2,256]{2,1,0:T(2,128)} %copy-done.22) | copy-start | bytes 24580
  941.6 150.4 %copy-start.21 = (f32[4,2,256]{2,1,0:T(2,128)S(1)}, f32[4,2,256]{2,1,0:T(2,128)}, u32[]{:S(2)}) copy-start(f32[4,2,256]{2,1,0:T(2,128)} %copy-done.20) | copy-start | bytes 24580
  941.6 152.8 %copy-start.33 = (s32[1,2048]{1,0:T(1,128)S(1)}, s32[1,2048]{1,0:T(1,128)}, u32[]{:S(2)}) copy-start(s32[1,2048]{1,0:T(1,128)} %copy-done.32) | copy-start | bytes 24580
  941.6 152.8 %copy-start.53 = (f32[1,1024]{1,0:T(1,128)S(1)}, f32[1,1024]{1,0:T(1,128)}, u32[]{:S(2)}) copy-start(f32[1,1024]{1,0:T(1,128)} %get-tuple-element.132) | copy-start | bytes 12292
  941.7 152.8 %copy-start.54 = (f32[1,1024]{1,0:T(1,128)S(1)}, f32[1,1024]{1,0:T(1,128)}, u32[]{:S(2)}) copy-start(f32[1,1024]{1,0:T(1,128)} %get-tuple-element.133) | copy-start | bytes 12292
  1089.9 279.7 %collective-permute-start.34 = (f32[4000,2048]{1,0:T(8,128)}, f32[4000,2048]{1,0:T(8,128)}, u32[]{:S(2)}, u32[]{:S(2)}) collective-permute-start(f32[4000,2048]{1,0:T(8,128)} %fusion), channel_id=1, source_target_pairs={{0,1},{1,0},{2,3},{3,2},{4,5},{5,4},{6,7},{7,6}} | collective-permute-start | bytes 98304008 | tf_op jit(solution)/shard_map/ppermute | solution.py:161
  1092.1 93.8 %collective-permute-start.30 = (f32[512,2048]{1,0:T(8,128)}, f32[512,2048]{1,0:T(8,128)}, u32[]{:S(2)}, u32[]{:S(2)}) collective-permute-start(f32[512,2048]{1,0:T(8,128)} %get-tuple-element.118), channel_id=1, source_target_pairs={{0,2},{1,3},{2,0},{3,1},{4,6},{5,7},{6,4},{7,5}} | collective-permute-start | bytes 12582920 | tf_op jit(solution)/shard_map/ppermute | solution.py:161
  1093.0 93.8 %collective-permute-start.31 = (f32[512,2048]{1,0:T(8,128)}, f32[512,2048]{1,0:T(8,128)}, u32[]{:S(2)}, u32[]{:S(2)}) collective-permute-start(f32[512,2048]{1,0:T(8,128)} %get-tuple-element.119), channel_id=1, source_target_pairs={{0,4},{1,5},{2,6},{3,7},{4,0},{5,1},{6,2},{7,3}} | collective-permute-start | bytes 12582920 | tf_op jit(solution)/shard_map/ppermute | solution.py:161
  1104.9 126.8 %collective-permute-start.28 = (f32[256,2048]{1,0:T(8,128)S(1)}, f32[256,2048]{1,0:T(8,128)}, u32[]{:S(2)}, u32[]{:S(2)}) collective-permute-start(f32[256,2048]{1,0:T(8,128)S(1)} %copy-done.7), channel_id=1, source_target_pairs={{0,4},{1,5},{2,6},{3,7},{4,0},{5,1},{6,2},{7,3}} | collective-permute-start | bytes 6291464 | tf_op jit(solution)/shard_map/ppermute | solution.py:161
  1105.7 126.0 %collective-permute-start.29 = (f32[256,2048]{1,0:T(8,128)}, f32[256,2048]{1,0:T(8,128)}, u32[]{:S(2)}, u32[]{:S(2)}) collective-permute-start(f32[256,2048]{1,0:T(8,128)} %slice_add_fusion.6.refs_3_), channel_id=1, source_target_pairs={{0,2},{1,3},{2,0},{3,1},{4,6},{5,7},{6,4},{7,5}} | collective-permute-start | bytes 6291464 | tf_op jit(solution)/shard_map/ppermute | solution.py:161
  1190.0 124.7 %collective-permute-start.33 = (f32[256,2048]{1,0:T(8,128)}, f32[256,2048]{1,0:T(8,128)}, u32[]{:S(2)}, u32[]{:S(2)}) collective-permute-start(f32[256,2048]{1,0:T(8,128)} %slice_add_fusion.12), channel_id=1, source_target_pairs={{0,2},{1,3},{2,0},{3,1},{4,6},{5,7},{6,4},{7,5}} | collective-permute-start | bytes 6291464 | tf_op jit(solution)/shard_map/ppermute | solution.py:161
  1194.3 120.3 %collective-permute-start.32 = (f32[256,2048]{1,0:T(8,128)}, f32[256,2048]{1,0:T(8,128)}, u32[]{:S(2)}, u32[]{:S(2)}) collective-permute-start(f32[256,2048]{1,0:T(8,128)} %slice_add_fusion.13), channel_id=1, source_target_pairs={{0,4},{1,5},{2,6},{3,7},{4,0},{5,1},{6,2},{7,3}} | collective-permute-start | bytes 6291464 | tf_op jit(solution)/shard_map/ppermute | solution.py:161
  (61 other events, 1466.3 us)
Sparse Core Ops, SparseCore 0:
  9.5 50.0 all-gather.3

commit v2 on v1

--- a/solution.py
+++ b/solution.py
@@ -216,16 +216,19 @@
                 out.append((s * HF, block * CH + col, c * 4 * CH + POS[r, s] * HF, HF))
             return out
 
-        x_x = [hop(x_own[c], 2) for c in range(3)]
-        x_y = [hop(x_own[c], 4) for c in range(3)]
+        x_x = [hop(x_own[c], 2) for c in range(2)]
+        x_y = [hop(x_own[c], 4) for c in range(2)]
         l_own, lse_own, x_all = local_logits(core_arr, w2, x_own, [whole(c, OWN, c) for c in range(NCH)], None, [])
-        late = after(x_own[3], lse_own)
+        x_d = [hop(after(x_y[0], lse_own), 2), hop(after(x_x[1], lse_own), 4)]
+        late = after(x_own[2], lse_own)
         x_x.append(hop(late, 2))
         x_y.append(hop(late, 4))
-        x_d = [hop(after(x_y[c], lse_own), 2) if c % 2 == 0 else hop(after(x_x[c], lse_own), 4) for c in range(2)]
         l_1, lse_1, x_all = local_logits(
             core_arr, w2, [x_x[0], x_y[0], x_x[1], x_y[1]],
             [split(0, XN, 0), split(0, YN, 0), split(1, XN, 2), split(1, YN, 2)], x_all, [])
+        late = after(x_own[3], lse_1)
+        x_x.append(hop(late, 2))
+        x_y.append(hop(late, 4))
         x_d.append(hop(after(x_y[2], lse_1), 2))
         l_2, lse_2, x_all = local_logits(
             core_arr, w2, [x_d[0], x_d[1], x_x[2], x_y[2]],
@@ -275,8 +278,8 @@
                 deps_out = [lse_3] + forward(0)
             if c == 2:
                 deps_out = list(pending[0])
-            if c >= 2:
-                deps_keep = forward(c - 1)
+            if c == 3:
+                deps_out = forward(1)
             (a_xy, b_xy), (a_dg, b_dg) = l_xy[c], l_dg[c]
             dz_all, pk1, send_a, send_b = local_grads(
                 core_arr, w2, lab_c[c][:, :t], lse_c[c][:, :t], sc_c[c][:, :t], [(a_xy, CH, b_xy), (a_dg, CH, b_dg)], dz_all, 2 * c,
@@ -302,6 +305,7 @@
             return jnp.einsum("vt,td->vd", dz_all[rows, cols], x_all[cols], preferred_element_type=F32)
 
         every, head, rest = slice(None), slice(0, 2 * NCH * CH), slice(2 * NCH * CH, None)
+        forward(2)
         dz_all, *pending[1] = lax.optimization_barrier((dz_all, *pending[1]))
         dw_other = dw_part(slice(VD, None), every)
         arrived[3] = after(arrived[3], dw_other[:8, :128])
@@ -328,7 +332,7 @@
             dh.append((r * gn - h * r ** 3 * proj).astype(BF16))
         dz_all, dg = lax.optimization_barrier((dz_all, dg))
         grad_w = dw_part(slice(0, VD), rest) + (dw_mine + dw_other)
-        tail = lax.psum(jnp.concatenate([dg, jnp.full((128,), loss_sum, F32)]), AX)
+        tail = jnp.sum(lax.all_gather(jnp.concatenate([dg, jnp.full((128,), loss_sum, F32)]), AX), axis=0)
         grad_g = lax.dynamic_slice(tail, (me * (D // NDEV),), (D // NDEV,))
         loss_value = tail[D] / count
         return loss_value, jnp.concatenate(dh).reshape(nb, seq_len, D), grad_w, grad_g

time: 1470 us -> 1510 us (1.027)
  waiting for transfers between devices: 146 us -> 197 us
    ppermute x35, waiting for transfers between devices: 139 us -> 190 us  [hop(): return lax.ppermute(a, AX, [(d, d ^ bit) for d in range(NDEV)])]
    psum x1 -> x0, blocking collectives: 22.7 us -> none  [local_step(): tail = lax.psum(jnp.concatenate([dg, jnp.full((128,), loss_sum, F32)]), AX)]
  transfers between devices with their start and end apart: 36 -> 36, of which waited for: 6 -> 5; matrix products, arithmetic and copies ran while one was open for 13% -> 13% of each run, Pallas kernels for 54% -> 53%
where the time goes in v2:
time: 1510 us; the launch traced here: 1500 us
  Pallas kernels  790 us (52%)
  matrix products  306 us (20%)
  waiting for transfers between devices  197 us (13%)
  other arithmetic  96 us (6%)
  starting transfers between devices  36.7 us (2%)
  blocking collectives  24.9 us (2%)
  local copies, waits for them, and re-layouts  24.8 us (2%)
  between operations  22.5 us (1%)
    pallas_call x8, Pallas kernels, local_grads(): pl.pallas_call(functools.partial(grad_kernel, tuple((width for _, width,...  422 us
    pallas_call x4, Pallas kernels, local_logits(): pl.pallas_call(functools.partial(logits_kernel, moves, x_all is not None,...  368 us
    dot_general x3, matrix products, dw_part(): jnp.einsum('vt,td->vd', dz_all[rows, cols], x_all[cols], preferred_elemen...  306 us
    ppermute x35, waiting for transfers between devices, hop(): return lax.ppermute(a, AX, [(d, d ^ bit) for d in range(NDEV)])  190 us
    ppermute x35, starting transfers between devices, hop(): return lax.ppermute(a, AX, [(d, d ^ bit) for d in range(NDEV)])  36.6 us
  transfers between devices with their start and end apart: 36, of which 5 were waited for; matrix products, arithmetic and copies ran while one was open for 13% of the time, Pallas kernels for 53%

profile of v2, /device:TPU:0, one launch (start us, length us, event | category | flops | bytes accessed | tf_op | source)
XLA Modules:
  0.0 1498.0 jit_solution(12030920365027413840)
XLA Ops:
  8.0 13.9 all-gather.2
  21.9 7.6 fusion.42
  30.7 2.7 copy-done
  33.4 5.8 fusion.25
  39.6 1.5 collective-permute-start.2
  41.7 1.7 collective-permute-start
  53.3 6.3 all-gather.6.cloned.1.call-done.w_ref
  59.6 88.7 %shard_map.129 = (f32[8000,2048]{1,0:T(8,128)}, f32[1,2048]{1,0:T(1,128)}, bf16[8192,2048]{1,0:T(8,128)(2,1)}) custom-call(s32[1]{0:T(128)} %bitcast.core_ref, bf16[8000,2048]{1,0:T(8,128)(2,1)} %all-gather.6.cloned.1.call-done.w_ref, bf16[512,2048]{1,0:T(8,128)(2,1)} %get-tuple-element.177.refs_0_, bf16[512,2048]{1,0:T(8,128)(2,1)} %get-tuple-element.175.refs_1_, ...), custom_call_target="tpu_custom_call" | custom-call | flops 67108864000 | bytes 98304000 | tf_op jit(solution)/shard_map/pallas_call | solution.py:79
  148.3 1.8 collective-permute-start.5
  152.4 101.5 %shard_map.130 = (f32[8000,2048]{1,0:T(8,128)}, f32[1,2048]{1,0:T(1,128)}, bf16[8192,2048]{1,0:T(8,128)(2,1)}) custom-call(s32[1]{0:T(128)} %bitcast.core_ref, bf16[8000,2048]{1,0:T(8,128)(2,1)} %all-gather.6.cloned.1.call-done.w_ref, bf16[512,2048]{1,0:T(8,128)(2,1)} %collective-permute-done.6.refs_0_, ...), custom_call_target="tpu_custom_call", output_to_operand_aliasing={{2}: (6, {})} | custom-call | flops 67108864000 | bytes 98304000 | tf_op jit(solution)/shard_map/pallas_call | solution.py:79
  254.0 1.8 collective-permute-start.9
  257.1 88.8 %shard_map.131 = (f32[8000,2048]{1,0:T(8,128)}, f32[1,2048]{1,0:T(1,128)}, bf16[8192,2048]{1,0:T(8,128)(2,1)}) custom-call(s32[1]{0:T(128)} %bitcast.core_ref, bf16[8000,2048]{1,0:T(8,128)(2,1)} %all-gather.6.cloned.1.call-done.w_ref, bf16[512,2048]{1,0:T(8,128)(2,1)} %collective-permute-done.1.refs_0_, ...), custom_call_target="tpu_custom_call", output_to_operand_aliasing={{2}: (6, {})} | custom-call | flops 67108864000 | bytes 98304000 | tf_op jit(solution)/shard_map/pallas_call | solution.py:79
  347.4 1.5 collective-permute-start.13
  349.2 1.7 collective-permute-start.12
  351.0 1.5 collective-permute-start.11
  358.3 53.1 %shard_map.132 = (bf16[8000,8192]{1,0:T(8,128)(2,1)}, f32[1,1024]{1,0:T(1,128)}, f32[512,2048]{1,0:T(8,128)}, f32[512,2048]{1,0:T(8,128)}) custom-call(s32[1]{0:T(128)} %bitcast.core_ref, bf16[8000,2048]{1,0:T(8,128)(2,1)} %all-gather.6.cloned.1.call-done.w_ref, s32[1,1024]{1,0:T(1,128)} %get-tuple-element.302.lab_ref, ...), custom_call_target="tpu_custom_call" | custom-call | flops 33554432000 | bytes 81920000 | tf_op jit(solution)/shard_map/pallas_call | solution.py:144
  411.4 1.8 collective-permute-start.18
  414.6 52.7 %shard_map.133 = (bf16[8000,8192]{1,0:T(8,128)(2,1)}, f32[1,1024]{1,0:T(1,128)}, f32[256,2048]{1,0:T(8,128)}, f32[256,2048]{1,0:T(8,128)}, f32[512,2048]{1,0:T(8,128)}) custom-call(s32[1]{0:T(128)} %bitcast.core_ref, bf16[8000,2048]{1,0:T(8,128)(2,1)} %all-gather.6.cloned.1.call-done.w_ref, ...), custom_call_target="tpu_custom_call", output_to_operand_aliasing={{0}: (7, {})} | custom-call | flops 33554432000 | bytes 81920000 | tf_op jit(solution)/shard_map/pallas_call | solution.py:144
  467.5 88.9 %shard_map.134 = (f32[8000,2048]{1,0:T(8,128)}, f32[1,2048]{1,0:T(1,128)}, bf16[8192,2048]{1,0:T(8,128)(2,1)}) custom-call(s32[1]{0:T(128)} %bitcast.core_ref, bf16[8000,2048]{1,0:T(8,128)(2,1)} %all-gather.6.cloned.1.call-done.w_ref, bf16[512,2048]{1,0:T(8,128)(2,1)} %collective-permute-done.8.refs_0_, ...), custom_call_target="tpu_custom_call", output_to_operand_aliasing={{2}: (7, {})} | custom-call | flops 67108864000 | bytes 98304000 | tf_op jit(solution)/shard_map/pallas_call | solution.py:79
  566.0 3.9 slice_add_fusion.10.refs_4_
  571.1 3.2 slice_add_fusion.11.refs_3_
  575.0 52.7 %shard_map.135 = (bf16[8000,8192]{1,0:T(8,128)(2,1)}, f32[1,1024]{1,0:T(1,128)}, f32[512,2048]{1,0:T(8,128)}, f32[512,2048]{1,0:T(8,128)}) custom-call(s32[1]{0:T(128)} %bitcast.core_ref, bf16[8000,2048]{1,0:T(8,128)(2,1)} %all-gather.6.cloned.1.call-done.w_ref, s32[1,1024]{1,0:T(1,128)} %get-tuple-element.226.lab_ref, ...), custom_call_target="tpu_custom_call", output_to_operand_aliasing={{0}: (10, {})} | custom-call | flops 33554432000 | bytes 81920000 | tf_op jit(solution)/shard_map/pallas_call | solution.py:144
  629.9 52.5 %shard_map.136 = (bf16[8000,8192]{1,0:T(8,128)(2,1)}, f32[1,1024]{1,0:T(1,128)}, f32[256,2048]{1,0:T(8,128)}, f32[256,2048]{1,0:T(8,128)}, f32[512,2048]{1,0:T(8,128)}) custom-call(s32[1]{0:T(128)} %bitcast.core_ref, bf16[8000,2048]{1,0:T(8,128)(2,1)} %all-gather.6.cloned.1.call-done.w_ref, ...), custom_call_target="tpu_custom_call", output_to_operand_aliasing={{0}: (7, {})} | custom-call | flops 33554432000 | bytes 81920000 | tf_op jit(solution)/shard_map/pallas_call | solution.py:144
  682.4 52.7 %shard_map.137 = (bf16[8000,8192]{1,0:T(8,128)(2,1)}, f32[1,1024]{1,0:T(1,128)}, f32[512,2048]{1,0:T(8,128)}, f32[512,2048]{1,0:T(8,128)}) custom-call(s32[1]{0:T(128)} %bitcast.core_ref, bf16[8000,2048]{1,0:T(8,128)(2,1)} %all-gather.6.cloned.1.call-done.w_ref, s32[1,1024]{1,0:T(1,128)} %get-tuple-element.196.lab_ref, ...), custom_call_target="tpu_custom_call", output_to_operand_aliasing={{0}: (9, {})} | custom-call | flops 33554432000 | bytes 81920000 | tf_op jit(solution)/shard_map/pallas_call | solution.py:144
  735.1 52.6 %shard_map.138 = (bf16[8000,8192]{1,0:T(8,128)(2,1)}, f32[1,1024]{1,0:T(1,128)}, f32[256,2048]{1,0:T(8,128)}, f32[256,2048]{1,0:T(8,128)}, f32[512,2048]{1,0:T(8,128)}) custom-call(s32[1]{0:T(128)} %bitcast.core_ref, bf16[8000,2048]{1,0:T(8,128)(2,1)} %all-gather.6.cloned.1.call-done.w_ref, ...), custom_call_target="tpu_custom_call", output_to_operand_aliasing={{0}: (7, {})} | custom-call | flops 33554432000 | bytes 81920000 | tf_op jit(solution)/shard_map/pallas_call | solution.py:144
  787.8 4.1 slice_add_fusion.9.refs_2_
  793.2 3.2 slice_add_fusion.8.refs_3_
  796.9 53.1 %shard_map.139 = (bf16[8000,8192]{1,0:T(8,128)(2,1)}, f32[1,1024]{1,0:T(1,128)}, f32[512,2048]{1,0:T(8,128)}, f32[512,2048]{1,0:T(8,128)}) custom-call(s32[1]{0:T(128)} %bitcast.core_ref, bf16[8000,2048]{1,0:T(8,128)(2,1)} %all-gather.6.cloned.1.call-done.w_ref, s32[1,1024]{1,0:T(1,128)} %get-tuple-element.256.lab_ref, ...), custom_call_target="tpu_custom_call", output_to_operand_aliasing={{0}: (9, {})} | custom-call | flops 33554432000 | bytes 81920000 | tf_op jit(solution)/shard_map/pallas_call | solution.py:144
  850.0 52.8 %shard_map.140 = (bf16[8000,8192]{1,0:T(8,128)(2,1)}, f32[1,1024]{1,0:T(1,128)}, f32[256,2048]{1,0:T(8,128)}, f32[256,2048]{1,0:T(8,128)}, f32[512,2048]{1,0:T(8,128)}) custom-call(s32[1]{0:T(128)} %bitcast.core_ref, bf16[8000,2048]{1,0:T(8,128)(2,1)} %all-gather.6.cloned.1.call-done.w_ref, ...), custom_call_target="tpu_custom_call", output_to_operand_aliasing={{0}: (7, {})} | custom-call | flops 33554432000 | bytes 81920000 | tf_op jit(solution)/shard_map/pallas_call | solution.py:144
  903.0 148.2 %fusion = f32[4000,2048]{1,0:T(8,128)} fusion(bf16[8192,2048]{1,0:T(8,128)(2,1)} %get-tuple-element.141, bf16[8000,8192]{1,0:T(8,128)(2,1)} %get-tuple-element.140), kind=kOutput, calls=%fused_computation.7 | convolution fusion | flops 134217728000 | bytes 131858432 | tf_op jit(solution)/shard_map/vt,td->vd/dot_general | solution.py:305
  1059.5 7.3 fusion.57
  1066.7 79.0 %collective-permute-done.26 = f32[512,2048]{1,0:T(8,128)} collective-permute-done((f32[512,2048]{1,0:T(8,128)}, f32[512,2048]{1,0:T(8,128)}, u32[]{:S(2)}, u32[]{:S(2)}) %collective-permute-start.26) | collective-permute-done | bytes 4194336 | tf_op jit(solution)/shard_map/ppermute | solution.py:161
  1145.7 3.1 slice_add_fusion.2
  1150.2 3.2 slice_add_fusion.1
  1155.6 7.2 fusion.53
  1162.8 72.8 %collective-permute-done.30 = f32[512,2048]{1,0:T(8,128)} collective-permute-done((f32[512,2048]{1,0:T(8,128)}, f32[512,2048]{1,0:T(8,128)}, u32[]{:S(2)}, u32[]{:S(2)}) %collective-permute-start.30) | collective-permute-done | bytes 4194336 | tf_op jit(solution)/shard_map/ppermute | solution.py:161
  1237.1 3.2 slice_add_fusion.12
  1241.0 3.2 slice_add_fusion.13
  1245.4 36.5 %collective-permute-done.27 = f32[256,2048]{1,0:T(8,128)S(1)} collective-permute-done((f32[256,2048]{1,0:T(8,128)}, f32[256,2048]{1,0:T(8,128)S(1)}, u32[]{:S(2)}, u32[]{:S(2)}) %collective-permute-start.27) | collective-permute-done | bytes 2097184 | tf_op jit(solution)/shard_map/ppermute | solution.py:161
  1281.9 77.6 %fusion.2 = f32[4000,2048]{1,0:T(8,128)} fusion(bf16[8000,8192]{1,0:T(8,128)(2,1)} %get-tuple-element.140, bf16[8192,2048]{1,0:T(8,128)(2,1)} %get-tuple-element.141), kind=kOutput, calls=%fused_computation.10 | convolution fusion | flops 67108864000 | bytes 82313216 | tf_op jit(solution)/shard_map/vt,td->vd/dot_general | solution.py:305
  1359.6 5.9 fusion.49
  1365.6 5.4 add_convert_fusion.1
  1371.3 5.9 fusion.41
  1377.3 6.7 fusion.33
  1384.0 11.1 all-gather.3
  1397.7 7.6 fusion.21
  1405.3 4.0 pad_maximum_fusion
  1409.3 80.3 %add_add_fusion = f32[4000,2048]{1,0:T(8,128)} fusion(f32[4000,2048]{1,0:T(8,128)} %fusion.2, f32[4000,2048]{1,0:T(8,128)} %collective-permute-done.34, bf16[8000,8192]{1,0:T(8,128)(2,1)} %get-tuple-element.140, bf16[8192,2048]{1,0:T(8,128)(2,1)} %get-tuple-element.141), kind=kOutput, calls=%fused_computation.9 | convolution fusion | flops 67125248000 | bytes 147849216 | tf_op jit(solution)/shard_map/vt,td->vd/dot_general | solution.py:305
  (481 shorter events, 53.2 us)
Async XLA Ops:
  7.2 52.4 %all-gather.6.cloned.1.call-start = ((), (), s32[]{:S(2)}) async-start(), calls=%async_computation | async-start | bytes 49152000 | tf_op jit(solution)/shard_map/all_gather | solution.py:190
  39.3 112.8 %collective-permute-start.7 = (bf16[512,2048]{1,0:T(8,128)(2,1)}, bf16[512,2048]{1,0:T(8,128)(2,1)}, u32[]{:S(2)}, u32[]{:S(2)}) collective-permute-start(bf16[512,2048]{1,0:T(8,128)(2,1)} %get-tuple-element.175.refs_1_), channel_id=1, source_target_pairs={{0,4},{1,5},{2,6},{3,7},{4,0},{5,1},{6,2},{7,3}} | collective-permute-start | bytes 6291464 | tf_op jit(solution)/shard_map/ppermute | solution.py:161
  39.6 110.5 %collective-permute-start.2 = (bf16[512,2048]{1,0:T(8,128)(2,1)}, bf16[512,2048]{1,0:T(8,128)(2,1)}, u32[]{:S(2)}, u32[]{:S(2)}) collective-permute-start(bf16[512,2048]{1,0:T(8,128)(2,1)} %get-tuple-element.175.refs_1_), channel_id=1, source_target_pairs={{0,2},{1,3},{2,0},{3,1},{4,6},{5,7},{6,4},{7,5}} | collective-permute-start | bytes 6291464 | tf_op jit(solution)/shard_map/ppermute | solution.py:161
  41.1 111.3 %collective-permute-start.6 = (bf16[512,2048]{1,0:T(8,128)(2,1)}, bf16[512,2048]{1,0:T(8,128)(2,1)}, u32[]{:S(2)}, u32[]{:S(2)}) collective-permute-start(bf16[512,2048]{1,0:T(8,128)(2,1)} %get-tuple-element.177.refs_0_), channel_id=1, source_target_pairs={{0,2},{1,3},{2,0},{3,1},{4,6},{5,7},{6,4},{7,5}} | collective-permute-start | bytes 6291464 | tf_op jit(solution)/shard_map/ppermute | solution.py:161
  41.7 109.9 %collective-permute-start = (bf16[512,2048]{1,0:T(8,128)(2,1)}, bf16[512,2048]{1,0:T(8,128)(2,1)}, u32[]{:S(2)}, u32[]{:S(2)}) collective-permute-start(bf16[512,2048]{1,0:T(8,128)(2,1)} %get-tuple-element.177.refs_0_), channel_id=1, source_target_pairs={{0,4},{1,5},{2,6},{3,7},{4,0},{5,1},{6,2},{7,3}} | collective-permute-start | bytes 6291464 | tf_op jit(solution)/shard_map/ppermute | solution.py:161
  148.3 108.8 %collective-permute-start.5 = (bf16[512,2048]{1,0:T(8,128)(2,1)}, bf16[512,2048]{1,0:T(8,128)(2,1)}, u32[]{:S(2)}, u32[]{:S(2)}) collective-permute-start(bf16[512,2048]{1,0:T(8,128)(2,1)} %get-tuple-element.76.refs_2_), channel_id=1, source_target_pairs={{0,4},{1,5},{2,6},{3,7},{4,0},{5,1},{6,2},{7,3}} | collective-permute-start | bytes 6291464 | tf_op jit(solution)/shard_map/ppermute | solution.py:161
  150.1 107.0 %collective-permute-start.4 = (bf16[512,2048]{1,0:T(8,128)(2,1)}, bf16[512,2048]{1,0:T(8,128)(2,1)}, u32[]{:S(2)}, u32[]{:S(2)}) collective-permute-start(bf16[512,2048]{1,0:T(8,128)(2,1)} %get-tuple-element.76.refs_2_), channel_id=1, source_target_pairs={{0,2},{1,3},{2,0},{3,1},{4,6},{5,7},{6,4},{7,5}} | collective-permute-start | bytes 6291464 | tf_op jit(solution)/shard_map/ppermute | solution.py:161
  151.6 105.5 %collective-permute-start.1 = (bf16[512,2048]{1,0:T(8,128)(2,1)}, bf16[512,2048]{1,0:T(8,128)(2,1)}, u32[]{:S(2)}, u32[]{:S(2)}) collective-permute-start(bf16[512,2048]{1,0:T(8,128)(2,1)} %collective-permute-done.refs_1_), channel_id=1, source_target_pairs={{0,2},{1,3},{2,0},{3,1},{4,6},{5,7},{6,4},{7,5}} | collective-permute-start | bytes 6291464 | tf_op jit(solution)/shard_map/ppermute | solution.py:161
  152.1 105.0 %collective-permute-start.3 = (bf16[512,2048]{1,0:T(8,128)(2,1)}, bf16[512,2048]{1,0:T(8,128)(2,1)}, u32[]{:S(2)}, u32[]{:S(2)}) collective-permute-start(bf16[512,2048]{1,0:T(8,128)(2,1)} %collective-permute-done.2.refs_2_), channel_id=1, source_target_pairs={{0,4},{1,5},{2,6},{3,7},{4,0},{5,1},{6,2},{7,3}} | collective-permute-start | bytes 6291464 | tf_op jit(solution)/shard_map/ppermute | solution.py:161
  254.0 98.5 %collective-permute-start.9 = (bf16[512,2048]{1,0:T(8,128)(2,1)}, bf16[512,2048]{1,0:T(8,128)(2,1)}, u32[]{:S(2)}, u32[]{:S(2)}) collective-permute-start(bf16[512,2048]{1,0:T(8,128)(2,1)} %get-tuple-element.82.refs_3_), channel_id=1, source_target_pairs={{0,2},{1,3},{2,0},{3,1},{4,6},{5,7},{6,4},{7,5}} | collective-permute-start | bytes 6291464 | tf_op jit(solution)/shard_map/ppermute | solution.py:161
  347.4 5.6 collective-permute-start.13
  348.9 5.1 collective-permute-start.14
  349.2 5.6 collective-permute-start.12
  351.0 116.4 %collective-permute-start.11 = (bf16[512,2048]{1,0:T(8,128)(2,1)}, bf16[512,2048]{1,0:T(8,128)(2,1)}, u32[]{:S(2)}, u32[]{:S(2)}) collective-permute-start(bf16[512,2048]{1,0:T(8,128)(2,1)} %get-tuple-element.82.refs_3_), channel_id=1, source_target_pairs={{0,4},{1,5},{2,6},{3,7},{4,0},{5,1},{6,2},{7,3}} | collective-permute-start | bytes 6291464 | tf_op jit(solution)/shard_map/ppermute | solution.py:161
  352.5 114.9 %collective-permute-start.8 = (bf16[512,2048]{1,0:T(8,128)(2,1)}, bf16[512,2048]{1,0:T(8,128)(2,1)}, u32[]{:S(2)}, u32[]{:S(2)}) collective-permute-start(bf16[512,2048]{1,0:T(8,128)(2,1)} %collective-permute-done.5.refs_3_), channel_id=1, source_target_pairs={{0,2},{1,3},{2,0},{3,1},{4,6},{5,7},{6,4},{7,5}} | collective-permute-start | bytes 6291464 | tf_op jit(solution)/shard_map/ppermute | solution.py:161
  353.0 114.3 %collective-permute-start.10 = (bf16[512,2048]{1,0:T(8,128)(2,1)}, bf16[512,2048]{1,0:T(8,128)(2,1)}, u32[]{:S(2)}, u32[]{:S(2)}) collective-permute-start(bf16[512,2048]{1,0:T(8,128)(2,1)} %collective-permute-done.9.refs_2_), channel_id=1, source_target_pairs={{0,4},{1,5},{2,6},{3,7},{4,0},{5,1},{6,2},{7,3}} | collective-permute-start | bytes 6291464 | tf_op jit(solution)/shard_map/ppermute | solution.py:161
  411.4 159.7 %collective-permute-start.18 = (f32[512,2048]{1,0:T(8,128)}, f32[512,2048]{1,0:T(8,128)}, u32[]{:S(2)}, u32[]{:S(2)}) collective-permute-start(f32[512,2048]{1,0:T(8,128)} %get-tuple-element.93), channel_id=1, source_target_pairs={{0,2},{1,3},{2,0},{3,1},{4,6},{5,7},{6,4},{7,5}} | collective-permute-start | bytes 12582920 | tf_op jit(solution)/shard_map/ppermute | solution.py:161
  413.1 152.9 %collective-permute-start.19 = (f32[512,2048]{1,0:T(8,128)}, f32[512,2048]{1,0:T(8,128)}, u32[]{:S(2)}, u32[]{:S(2)}) collective-permute-start(f32[512,2048]{1,0:T(8,128)} %get-tuple-element.95), channel_id=1, source_target_pairs={{0,4},{1,5},{2,6},{3,7},{4,0},{5,1},{6,2},{7,3}} | collective-permute-start | bytes 12582920 | tf_op jit(solution)/shard_map/ppermute | solution.py:161
  557.5 4.7 collective-permute-start.16
  558.1 4.8 collective-permute-start.17
  559.5 4.1 collective-permute-start.15
  570.0 112.4 %collective-permute-start.23 = (f32[256,2048]{1,0:T(8,128)}, f32[256,2048]{1,0:T(8,128)}, u32[]{:S(2)}, u32[]{:S(2)}) collective-permute-start(f32[256,2048]{1,0:T(8,128)} %slice_add_fusion.10.refs_4_), channel_id=1, source_target_pairs={{0,2},{1,3},{2,0},{3,1},{4,6},{5,7},{6,4},{7,5}} | collective-permute-start | bytes 6291464 | tf_op jit(solution)/shard_map/ppermute | solution.py:161
  574.2 108.2 %collective-permute-start.22 = (f32[256,2048]{1,0:T(8,128)}, f32[256,2048]{1,0:T(8,128)}, u32[]{:S(2)}, u32[]{:S(2)}) collective-permute-start(f32[256,2048]{1,0:T(8,128)} %slice_add_fusion.11.refs_3_), channel_id=1, source_target_pairs={{0,4},{1,5},{2,6},{3,7},{4,0},{5,1},{6,2},{7,3}} | collective-permute-start | bytes 6291464 | tf_op jit(solution)/shard_map/ppermute | solution.py:161
  627.7 160.1 %collective-permute-start.20 = (f32[512,2048]{1,0:T(8,128)}, f32[512,2048]{1,0:T(8,128)}, u32[]{:S(2)}, u32[]{:S(2)}) collective-permute-start(f32[512,2048]{1,0:T(8,128)} %get-tuple-element.99), channel_id=1, source_target_pairs={{0,2},{1,3},{2,0},{3,1},{4,6},{5,7},{6,4},{7,5}} | collective-permute-start | bytes 12582920 | tf_op jit(solution)/shard_map/ppermute | solution.py:161
  629.1 164.0 %collective-permute-start.21 = (f32[512,2048]{1,0:T(8,128)}, f32[512,2048]{1,0:T(8,128)}, u32[]{:S(2)}, u32[]{:S(2)}) collective-permute-start(f32[512,2048]{1,0:T(8,128)} %get-tuple-element.101), channel_id=1, source_target_pairs={{0,4},{1,5},{2,6},{3,7},{4,0},{5,1},{6,2},{7,3}} | collective-permute-start | bytes 12582920 | tf_op jit(solution)/shard_map/ppermute | solution.py:161
  791.9 110.9 %collective-permute-start.24 = (f32[256,2048]{1,0:T(8,128)}, f32[256,2048]{1,0:T(8,128)}, u32[]{:S(2)}, u32[]{:S(2)}) collective-permute-start(f32[256,2048]{1,0:T(8,128)} %slice_add_fusion.9.refs_2_), channel_id=1, source_target_pairs={{0,4},{1,5},{2,6},{3,7},{4,0},{5,1},{6,2},{7,3}} | collective-permute-start | bytes 6291464 | tf_op jit(solution)/shard_map/ppermute | solution.py:161
  796.4 106.5 %collective-permute-start.25 = (f32[256,2048]{1,0:T(8,128)}, f32[256,2048]{1,0:T(8,128)}, u32[]{:S(2)}, u32[]{:S(2)}) collective-permute-start(f32[256,2048]{1,0:T(8,128)} %slice_add_fusion.8.refs_3_), channel_id=1, source_target_pairs={{0,2},{1,3},{2,0},{3,1},{4,6},{5,7},{6,4},{7,5}} | collective-permute-start | bytes 6291464 | tf_op jit(solution)/shard_map/ppermute | solution.py:161
  902.9 148.4 %copy-start.38 = (f32[1,2048]{1,0:T(1,128)S(1)}, f32[1,2048]{1,0:T(1,128)}, u32[]{:S(2)}) copy-start(f32[1,2048]{1,0:T(1,128)} %copy-done.37) | copy-start | bytes 24580
  902.9 148.4 %copy-start.40 = (s32[1,2048]{1,0:T(1,128)S(1)}, s32[1,2048]{1,0:T(1,128)}, u32[]{:S(2)}) copy-start(s32[1,2048]{1,0:T(1,128)} %copy-done.39) | copy-start | bytes 24580
  902.9 148.4 %copy-start.52 = (f32[1,1024]{1,0:T(1,128)S(1)}, f32[1,1024]{1,0:T(1,128)}, u32[]{:S(2)}) copy-start(f32[1,1024]{1,0:T(1,128)} %get-tuple-element.133) | copy-start | bytes 12292
  902.9 148.4 %copy-start.53 = (f32[1,1024]{1,0:T(1,128)S(1)}, f32[1,1024]{1,0:T(1,128)}, u32[]{:S(2)}) copy-start(f32[1,1024]{1,0:T(1,128)} %get-tuple-element.88.refs_4_) | copy-start | bytes 12292
  902.9 149.1 %copy-start.23 = (f32[4,2,256]{2,1,0:T(2,128)S(1)}, f32[4,2,256]{2,1,0:T(2,128)}, u32[]{:S(2)}) copy-start(f32[4,2,256]{2,1,0:T(2,128)} %copy-done.22) | copy-start | bytes 24580
  902.9 150.5 %copy-start.21 = (f32[4,2,256]{2,1,0:T(2,128)S(1)}, f32[4,2,256]{2,1,0:T(2,128)}, u32[]{:S(2)}) copy-start(f32[4,2,256]{2,1,0:T(2,128)} %copy-done.20) | copy-start | bytes 24580
  902.9 153.3 %copy-start.36 = (s32[1,2048]{1,0:T(1,128)S(1)}, s32[1,2048]{1,0:T(1,128)}, u32[]{:S(2)}) copy-start(s32[1,2048]{1,0:T(1,128)} %copy-done.35) | copy-start | bytes 24580
  902.9 153.3 %copy-start.54 = (f32[1,1024]{1,0:T(1,128)S(1)}, f32[1,1024]{1,0:T(1,128)}, u32[]{:S(2)}) copy-start(f32[1,1024]{1,0:T(1,128)} %get-tuple-element.134) | copy-start | bytes 12292
  902.9 153.3 %copy-start.55 = (f32[1,1024]{1,0:T(1,128)S(1)}, f32[1,1024]{1,0:T(1,128)}, u32[]{:S(2)}) copy-start(f32[1,1024]{1,0:T(1,128)} %get-tuple-element.135) | copy-start | bytes 12292
  902.9 155.2 %copy-start.34 = (s32[1,2048]{1,0:T(1,128)S(1)}, s32[1,2048]{1,0:T(1,128)}, u32[]{:S(2)}) copy-start(s32[1,2048]{1,0:T(1,128)} %copy-done.33) | copy-start | bytes 24580
  903.0 155.2 %copy-start.56 = (f32[1,1024]{1,0:T(1,128)S(1)}, f32[1,1024]{1,0:T(1,128)}, u32[]{:S(2)}) copy-start(f32[1,1024]{1,0:T(1,128)} %get-tuple-element.136) | copy-start | bytes 12292
  903.0 155.2 %copy-start.58 = (f32[1,1024]{1,0:T(1,128)S(1)}, f32[1,1024]{1,0:T(1,128)}, u32[]{:S(2)}) copy-start(f32[1,1024]{1,0:T(1,128)} %get-tuple-element.137) | copy-start | bytes 12292
  1051.2 358.1 %collective-permute-start.34 = (f32[4000,2048]{1,0:T(8,128)}, f32[4000,2048]{1,0:T(8,128)}, u32[]{:S(2)}, u32[]{:S(2)}) collective-permute-start(f32[4000,2048]{1,0:T(8,128)} %fusion), channel_id=1, source_target_pairs={{0,1},{1,0},{2,3},{3,2},{4,5},{5,4},{6,7},{7,6}} | collective-permute-start | bytes 98304008 | tf_op jit(solution)/shard_map/ppermute | solution.py:161
  1052.0 93.8 %collective-permute-start.26 = (f32[512,2048]{1,0:T(8,128)}, f32[512,2048]{1,0:T(8,128)}, u32[]{:S(2)}, u32[]{:S(2)}) collective-permute-start(f32[512,2048]{1,0:T(8,128)} %get-tuple-element.113), channel_id=1, source_target_pairs={{0,2},{1,3},{2,0},{3,1},{4,6},{5,7},{6,4},{7,5}} | collective-permute-start | bytes 12582920 | tf_op jit(solution)/shard_map/ppermute | solution.py:161
  1053.4 96.8 %collective-permute-start.28 = (f32[512,2048]{1,0:T(8,128)}, f32[512,2048]{1,0:T(8,128)}, u32[]{:S(2)}, u32[]{:S(2)}) collective-permute-start(f32[512,2048]{1,0:T(8,128)} %get-tuple-element.117), channel_id=1, source_target_pairs={{0,4},{1,5},{2,6},{3,7},{4,0},{5,1},{6,2},{7,3}} | collective-permute-start | bytes 12582920 | tf_op jit(solution)/shard_map/ppermute | solution.py:161
  1054.3 181.3 %collective-permute-start.30 = (f32[512,2048]{1,0:T(8,128)}, f32[512,2048]{1,0:T(8,128)}, u32[]{:S(2)}, u32[]{:S(2)}) collective-permute-start(f32[512,2048]{1,0:T(8,128)} %get-tuple-element.120), channel_id=1, source_target_pairs={{0,2},{1,3},{2,0},{3,1},{4,6},{5,7},{6,4},{7,5}} | collective-permute-start | bytes 12582920 | tf_op jit(solution)/shard_map/ppermute | solution.py:161
  1055.4 181.7 %collective-permute-start.31 = (f32[512,2048]{1,0:T(8,128)}, f32[512,2048]{1,0:T(8,128)}, u32[]{:S(2)}, u32[]{:S(2)}) collective-permute-start(f32[512,2048]{1,0:T(8,128)} %get-tuple-element.121), channel_id=1, source_target_pairs={{0,4},{1,5},{2,6},{3,7},{4,0},{5,1},{6,2},{7,3}} | collective-permute-start | bytes 12582920 | tf_op jit(solution)/shard_map/ppermute | solution.py:161
  1148.9 133.0 %collective-permute-start.27 = (f32[256,2048]{1,0:T(8,128)}, f32[256,2048]{1,0:T(8,128)S(1)}, u32[]{:S(2)}, u32[]{:S(2)}) collective-permute-start(f32[256,2048]{1,0:T(8,128)} %slice_add_fusion.2), channel_id=1, source_target_pairs={{0,4},{1,5},{2,6},{3,7},{4,0},{5,1},{6,2},{7,3}} | collective-permute-start | bytes 6291464 | tf_op jit(solution)/shard_map/ppermute | solution.py:161
  1153.4 128.5 %collective-permute-start.29 = (f32[256,2048]{1,0:T(8,128)}, f32[256,2048]{1,0:T(8,128)}, u32[]{:S(2)}, u32[]{:S(2)}) collective-permute-start(f32[256,2048]{1,0:T(8,128)} %slice_add_fusion.1), channel_id=1, source_target_pairs={{0,2},{1,3},{2,0},{3,1},{4,6},{5,7},{6,4},{7,5}} | collective-permute-start | bytes 6291464 | tf_op jit(solution)/shard_map/ppermute | solution.py:161
  1240.3 125.3 %collective-permute-start.33 = (f32[256,2048]{1,0:T(8,128)}, f32[256,2048]{1,0:T(8,128)}, u32[]{:S(2)}, u32[]{:S(2)}) collective-permute-start(f32[256,2048]{1,0:T(8,128)} %slice_add_fusion.12), channel_id=1, source_target_pairs={{0,2},{1,3},{2,0},{3,1},{4,6},{5,7},{6,4},{7,5}} | collective-permute-start | bytes 6291464 | tf_op jit(solution)/shard_map/ppermute | solution.py:161
  1244.1 121.5 %collective-permute-start.32 = (f32[256,2048]{1,0:T(8,128)}, f32[256,2048]{1,0:T(8,128)}, u32[]{:S(2)}, u32[]{:S(2)}) collective-permute-start(f32[256,2048]{1,0:T(8,128)} %slice_add_fusion.13), channel_id=1, source_target_pairs={{0,4},{1,5},{2,6},{3,7},{4,0},{5,1},{6,2},{7,3}} | collective-permute-start | bytes 6291464 | tf_op jit(solution)/shard_map/ppermute | solution.py:161
  (62 other events, 2130.3 us)
Sparse Core Ops, SparseCore 0:
  9.5 50.0 all-gather.5
